TPU v7x, 64 devices: a 2x2x8 block of a 4x4x8 slice. The times are simulated.
64 devices in a mesh: dp: 8 (over x, y, core), tp: 8 (over z).
Axes of the slice: x: 2, y: 2, z: 8, core: 2. Of those that a mesh axis runs over, the one named last changes fastest.
The devices are a block of a 4x4x8 slice.
Arguments:
- x: bfloat16 [512, 7168], P('dp'), parts along dimension 0
- k_cache: bfloat16 [512, 2048, 8, 128], P('dp', None, 'tp'), parts along dimension 0
- v_cache: bfloat16 [512, 2048, 8, 128], P('dp', None, 'tp'), parts along dimension 0
- gain_a: bfloat16 [7168], replicated
- wq: bfloat16 [7168, 7168], P(None, 'tp')
- wo: bfloat16 [7168, 7168], P('tp')
- gain_m: bfloat16 [7168], replicated
- w_gate: bfloat16 [7168, 20480], P(None, 'tp')
- w_up: bfloat16 [7168, 20480], P(None, 'tp')
- w_down: bfloat16 [20480, 7168], P('tp')
Outputs:
- output: bfloat16 [512, 7168], P('dp'), parts along dimension 0
There are 8 independent parts. A program takes and returns all parts, laid end to end along the dimension named above; an argument that names none is the same for every part.
All inputs are finite; a program needn't handle non-finite values.
Results may differ from a plain program's by a relative error of at most 0.017.
Values are sent between devices in bfloat16 or wider.
A program may use at most 768 MiB of HBM per device.

v0:
```python
import jax
import jax.numpy as jnp
from jax import lax
from jax.sharding import PartitionSpec as P

HEAD = 128
THETA = 10000


def normed(x, gain):
    wide = x.astype(jnp.float32)
    scale = lax.rsqrt(jnp.mean(wide * wide, -1, keepdims=True) + 1e-6)
    return (wide * scale * gain.astype(jnp.float32)).astype(jnp.bfloat16)


def turned(t, place, theta):
    half = t.shape[-1] // 2
    angle = place.astype(jnp.float32)[:, None] * theta ** (-jnp.arange(half, dtype=jnp.float32) / half)
    cos, sin = jnp.cos(angle)[:, None], jnp.sin(angle)[:, None]
    a, b = t[..., :half].astype(jnp.float32), t[..., half:].astype(jnp.float32)
    return jnp.concatenate([a * cos - b * sin, b * cos + a * sin], -1).astype(jnp.bfloat16)


def matmul(a, w):
    return jnp.dot(a, w, preferred_element_type=jnp.float32).astype(jnp.bfloat16)


def einsum(form, a, b):
    return jnp.einsum(form, a.astype(jnp.float32), b.astype(jnp.float32))


def seen_by(a, wq, k_cache, v_cache, head, theta):
    batch, cache, kv_heads = k_cache.shape[:3]
    place = jnp.full((batch,), cache - 1)
    q = turned(matmul(a, wq).reshape(batch, -1, head), place, theta).reshape(batch, kv_heads, -1, head)
    scores = einsum("bgsd,bugd->bgsu", q, k_cache) * head**-0.5
    weights = jax.nn.softmax(scores, -1).astype(jnp.bfloat16)
    return einsum("bgsu,bugd->bgsd", weights, v_cache).astype(jnp.bfloat16).reshape(batch, -1)


def hidden_of(b, w_gate, w_up):
    gate = jnp.dot(b, w_gate, preferred_element_type=jnp.float32)
    up = jnp.dot(b, w_up, preferred_element_type=jnp.float32)
    return (jax.nn.silu(gate) * up).astype(jnp.bfloat16)


def solution(mesh):
    def added(t, term):
        return (t.astype(jnp.float32) + lax.psum(term.astype(jnp.bfloat16), "tp").astype(jnp.float32)).astype(jnp.bfloat16)

    def step(x, k_cache, v_cache, gain_a, wq, wo, gain_m, w_gate, w_up, w_down):
        seen = seen_by(normed(x, gain_a), wq, k_cache, v_cache, HEAD, THETA)
        h = added(x, jnp.dot(seen, wo, preferred_element_type=jnp.float32))
        return added(h, jnp.dot(hidden_of(normed(h, gain_m), w_gate, w_up), w_down, preferred_element_type=jnp.float32))

    states, cache, columns, rows_of = P("dp", None), P("dp", None, "tp", None), P(None, "tp"), P("tp", None)
    return jax.shard_map(
        step,
        mesh=mesh,
        in_specs=(states, cache, cache, P(None), columns, rows_of, P(None), columns, columns, rows_of),
        out_specs=states,
        check_vma=False,
    )
```

profile of v0, /device:TPU:30, one launch (start us, length us, event | category | flops | bytes accessed | tf_op | source)
XLA Modules:
  0.0 247.3 jit_solution(12313400264384375550)
XLA Ops:
  6.5 0.0 all-reduce.3.cloned.1.call-start
  6.6 0.7 convert_element_type.66
  7.3 1.5 fusion.9
  8.8 7.3 %convolution_convert_fusion.2 = bf16[64,896]{1,0:T(8,128)(2,1)S(1)} fusion(bf16[7168,896]{1,0:T(8,128)(2,1)} %param.14, bf16[64,7168]{1,0:T(8,128)(2,1)} %param.10, f32[7168]{0:T(1024)S(1)} %convert_element_type.66, f32[64]{0:T(128)S(1)} %add_rsqrt_fusion.1), kind=kOutput, calls=%fused_computation.30 | convolution fusion | flops 823975936 | bytes 13906176 | tf_op jit(solution)/shard_map/dot_general | solution.py:25
  16.1 0.2 reshape.67
  16.3 0.1 fusion.30
  16.4 16.9 %fusion.48 = (f32[64,7]{1,0:T(8,128)S(1)}, f32[64,7,2048]{2,1,0:T(8,128)}) fusion(bf16[64,2048,1,128]{3,1,2,0:T(8,128)(2,1)} %param.11, bf16[64,7,64]{2,1,0:T(8,128)(2,1)S(1)} %get-tuple-element.8, bf16[64,7,64]{2,1,0:T(8,128)(2,1)S(1)} %get-tuple-element.7), kind=kOutput, calls=%fused_computation.61 | convolution fusion | flops 237864960 | bytes 37340928 | tf_op jit(solution)/shard_map/sub | solution.py:37
  33.3 14.1 %fusion.17 = bf16[64,7,128]{2,1,0:T(8,128)(2,1)S(1)} fusion(bf16[64,2048,1,128]{3,1,2,0:T(8,128)(2,1)} %param.12, f32[64,7,2048]{2,1,0:T(8,128)} %get-tuple-element.10, f32[64,7]{1,0:T(8,128)S(1)} %get-tuple-element.9), kind=kOutput, calls=%fused_computation.29 | convolution fusion | flops 236773376 | bytes 37340928 | tf_op jit(solution)/shard_map/bgsu,bugd->bgsd/dot_general | solution.py:29
  47.5 0.0 copy-start.1
  47.5 0.0 copy-start
  47.5 8.0 %convolution_convert_fusion = bf16[64,7168]{1,0:T(8,128)(2,1)} fusion(bf16[896,7168]{1,0:T(8,128)(2,1)} %param.15, bf16[8,8,7,128]{3,2,1,0:T(8,128)(2,1)S(1)} %bitcast.21), kind=kOutput, calls=%fused_computation.5 | convolution fusion | flops 822542336 | bytes 13877248 | tf_op jit(solution)/shard_map/dot_general | solution.py:53
  55.5 0.1 all-reduce.3.cloned.1.call-update
  55.6 0.2 all-reduce.5.cloned.1.call-start
  55.8 0.0 copy-done.1
  55.9 72.1 %all-reduce.3.cloned.1.call-done = bf16[64,7168]{1,0:T(8,128)(2,1)} async-done(((bf16[64,7168]{1,0:T(8,128)(2,1)}), bf16[64,7168]{1,0:T(8,128)(2,1)}) %all-reduce.3.cloned.1.call-update) | async-done | bytes 917520 | tf_op jit(solution)/shard_map/psum | solution.py:49
  127.9 0.0 copy-done
  127.9 1.6 fusion.13
  129.5 14.8 %fusion.35 = f32[64,2560]{1,0:T(8,128)S(1)} fusion(bf16[7168,2560]{1,0:T(8,128)(2,1)} %param.17, bf16[64,7168]{1,0:T(8,128)(2,1)S(1)} %get-tuple-element.6, f32[7168]{0:T(1024)S(1)} %convert_element_type.77, f32[64]{0:T(128)S(1)} %add_rsqrt_fusion), kind=kOutput, calls=%fused_computation.47 | convolution fusion | flops 2350645248 | bytes 38301952 | tf_op jit(solution)/shard_map/dot_general | solution.py:42
  144.4 26.6 %convolution_convert_fusion.1 = bf16[64,7168]{1,0:T(8,128)(2,1)} fusion(bf16[2560,7168]{1,0:T(8,128)(2,1)} %param.19, bf16[7168,2560]{1,0:T(8,128)(2,1)} %param.18, f32[64,2560]{1,0:T(8,128)S(1)} %fusion.35, bf16[64,7168]{1,0:T(8,128)(2,1)S(1)} %get-tuple-element.6, f32[7168]{0:T(1024)S(1)} %convert_element_type.77, f32[64]{0:T(128)S(1)} %add_rsqrt_fusion), kind=kOutput, calls=%fused_computation.6 | convolution fusion | flops 4700897280 | bytes 75919616 | tf_op jit(solution)/shard_map/dot_general | solution.py:54
  171.0 0.1 all-reduce.5.cloned.1.call-update
  171.0 67.1 %all-reduce.5.cloned.1.call-done = bf16[64,7168]{1,0:T(8,128)(2,1)} async-done(((bf16[64,7168]{1,0:T(8,128)(2,1)}), bf16[64,7168]{1,0:T(8,128)(2,1)}) %all-reduce.5.cloned.1.call-update) | async-done | bytes 917520 | tf_op jit(solution)/shard_map/psum | solution.py:49
  238.1 2.3 fusion.16
  (4 shorter events, 0.1 us)
Async XLA Ops:
  6.5 121.4 %all-reduce.3.cloned.1.call-start = ((), (), s32[]{:S(2)}) async-start(), calls=%async_computation | async-start | bytes 1835008 | tf_op jit(solution)/shard_map/psum | solution.py:49
  47.5 8.4 %copy-start.1 = (bf16[7168]{0:T(1024)(128)(2,1)S(1)}, bf16[7168]{0:T(1024)(128)(2,1)}, u32[]{:S(2)}) copy-start(bf16[7168]{0:T(1024)(128)(2,1)} %param.16) | copy-start | bytes 43012
  47.5 80.4 %copy-start = (bf16[64,7168]{1,0:T(8,128)(2,1)S(1)}, bf16[64,7168]{1,0:T(8,128)(2,1)}, u32[]{:S(2)}) copy-start(bf16[64,7168]{1,0:T(8,128)(2,1)} %param.10) | copy-start | bytes 2752516
  55.6 182.5 %all-reduce.5.cloned.1.call-start = ((), (), s32[]{:S(2)}) async-start(), calls=%async_computation.1 | async-start | bytes 1835008 | tf_op jit(solution)/shard_map/psum | solution.py:49
Sparse Core Ops, SparseCore 0:
  55.7 72.1 all-reduce.2
  171.2 66.9 all-reduce.4
where the time goes:
time: 248 us; the launch traced here: 247 us
  waiting for transfers between devices  139 us (56%)
  matrix products  87.8 us (35%)
  between operations  13.5 us (5%)
  other arithmetic  6.29 us (3%)
    psum x2, waiting for transfers between devices, added(): lax.psum(term.astype(jnp.bfloat16), 'tp').astype(jnp.float32)  139 us
    dot_general x1, matrix products, step(): jnp.dot(hidden_of(normed(h, gain_m), w_gate, w_up), w_down, preferred_ele...  26.6 us
    sub x1, matrix products, seen_by(): weights = jax.nn.softmax(scores, -1).astype(jnp.bfloat16)  16.9 us
    dot_general x1, matrix products, hidden_of(): gate = jnp.dot(b, w_gate, preferred_element_type=jnp.float32)  14.8 us
    dot_general x1, matrix products, einsum(): return jnp.einsum(form, a.astype(jnp.float32), b.astype(jnp.float32))  14.1 us
    dot_general x1, matrix products, step(): h = added(x, jnp.dot(seen, wo, preferred_element_type=jnp.float32))  8.02 us
    dot_general x1, matrix products, matmul(): jnp.dot(a, w, preferred_element_type=jnp.float32).astype(jnp.bfloat16)  7.29 us
  transfers between devices with their start and end apart: 2, of which 2 were waited for; matrix products, arithmetic and copies ran while one was open for 0% of the time, Pallas kernels for 0%

commit v1 on v0

v1 whole, which is shorter than its diff:
```python
import functools

import jax
import jax.numpy as jnp
import numpy as np
from jax import lax
from jax.experimental import pallas as pl
from jax.experimental.pallas import tpu as pltpu
from jax.sharding import PartitionSpec as P

HEAD = 128
THETA = 10000
MESH = pl.DeviceIdType.MESH
WIDE = 256
SLOTS = 10
KV_ITER = 4
KV_RING = 4

bf16, f32 = jnp.bfloat16, jnp.float32


def distance(k):
    odd = k % 2
    return 4 + odd * ((k + 1) // 2) - (1 - odd) * (k // 2)


def kernel(n, axis, x_ref, rot_ref, gain_a_ref, gain_m_ref, k_ref, v_ref, wq_ref, wo_ref, wg_ref, wu_ref, wd_ref, y_ref,
           kv, wbuf, act, hbuf, ybuf, term, hid, qh, oh,
           s1l, s1r, r1l, r1r, s2l, s2r, r2l, r2r,
           wsem, kvsem, dsem, ysem,
           s1l_s, s1l_r, s1r_s, s1r_r, g1l_s, g1l_r, g1r_s, g1r_r,
           s2l_s, s2l_r, s2r_s, s2r_r, g2l_s, g2l_r, g2r_s, g2r_r):
    me = lax.axis_index(axis)
    right, left = lax.rem(me + 1, n), lax.rem(me + n - 1, n)
    rows, dim = act.shape
    per = rows // n
    cache = k_ref.shape[1]
    q_cols = wq_ref.shape[1]
    heads = q_cols // HEAD
    ff = wg_ref.shape[1]
    own_cols = dim // n
    widths = [min(WIDE, own_cols - j) for j in range(0, own_cols, WIDE)]
    pairs = ff // WIDE
    iters = rows // KV_ITER
    wo_per = wbuf.shape[1] // q_cols
    wo_blocks = dim // WIDE

    def owner(k):
        return lax.rem(me + k, n)

    barrier = pltpu.get_barrier_semaphore()
    for other in (left, right):
        pl.semaphore_signal(barrier, inc=1, device_id={axis: other}, device_id_type=MESH)

    def wq_copy(b):
        w = min(WIDE, q_cols - b * WIDE)
        return pltpu.make_async_copy(wq_ref.at[:, pl.ds(b * WIDE, w)], wbuf.at[2 + b, :, pl.ds(0, w)], wsem.at[2 + b])

    q_blocks = -(-q_cols // WIDE)

    def wo_copy(t):
        return pltpu.make_async_copy(
            wo_ref.at[:, pl.ds(t * WIDE, WIDE)],
            wbuf.at[6 + t // wo_per, pl.ds((t % wo_per) * q_cols, q_cols), :],
            wsem.at[6 + t // wo_per])

    def first_row(it):
        k = it // 2
        return lax.rem(me + distance(k), n) * per + (it % 2) * KV_ITER

    def kv_copies(it):
        slot, base = it % KV_RING, (it % KV_RING) * (4 * cache)
        out = []
        for s in range(KV_ITER):
            for which, ref in enumerate((k_ref, v_ref)):
                row = pl.multiple_of(base + (2 * which + s // 2) * cache, cache)
                out.append(pltpu.make_async_copy(
                    ref.at[first_row(it) + s], kv.at[pl.ds(row, cache), pl.ds((s % 2) * HEAD, HEAD)], kvsem.at[slot]))
        return out

    def pair_copies(p):
        cols = pl.ds(pl.multiple_of(p * WIDE, WIDE), WIDE)
        slot = 2 * (p % (SLOTS // 2))
        return (pltpu.make_async_copy(wg_ref.at[:, cols], wbuf.at[slot], wsem.at[slot]),
                pltpu.make_async_copy(wu_ref.at[:, cols], wbuf.at[slot + 1], wsem.at[slot + 1]))

    phases = [(0,)] + [(i, i + 1) for i in range(1, n - 1, 2)] + [(n - 1,)]
    order = [(i, j) for ph in phases for j in range(len(widths)) for i in ph]
    in_kv = kv.shape[0] // ff
    per_slot = wbuf.shape[1] // ff

    def down_place(b):
        if b < in_kv:
            return kv.at[pl.ds(b * ff, ff), :]
        b -= in_kv
        return wbuf.at[b // per_slot, pl.ds((b % per_slot) * ff, ff), :]

    def column(o, j):
        return pl.multiple_of(o * own_cols + j * WIDE, HEAD)

    def down_copy(b):
        i, j = order[b]
        w = widths[j]
        return pltpu.make_async_copy(
            wd_ref.at[:, pl.ds(column(owner(distance(i)), j), w)], down_place(b).at[:, pl.ds(0, w)], dsem.at[b])

    for b in range(q_blocks):
        wq_copy(b).start()
    for it in range(KV_RING):
        for c in kv_copies(it):
            c.start()
    for t in range(wo_blocks):
        wo_copy(t).start()

    def normed_into(read, gain_ref):
        step = dim // 7
        for r in range(0, n, 2):
            total = jnp.zeros((2 * per, HEAD), f32)
            for c in range(0, dim, step):
                t = jnp.concatenate([read(r, c, step), read(r + 1, c, step)], 0)
                sq = t * t
                for l in range(0, step, HEAD):
                    total = total + sq[:, l:l + HEAD]
            scale = lax.rsqrt(jnp.sum(total, -1, keepdims=True) / dim + 1e-6)
            for c in range(0, dim, step):
                t = jnp.concatenate([read(r, c, step), read(r + 1, c, step)], 0)
                act[r * per:(r + 2) * per, c:c + step] = (t * scale * gain_ref[:, c:c + step].astype(f32)).astype(bf16)

    normed_into(lambda r, c, w: x_ref[r, :, c:c + w].astype(f32), gain_a_ref)

    qh[heads * rows:, :] = jnp.zeros((qh.shape[0] - heads * rows, HEAD), f32)
    for b in range(q_blocks):
        wq_copy(b).wait()
        w = min(WIDE, q_cols - b * WIDE)
        q = jnp.dot(act[...], wbuf[2 + b, :, :w], preferred_element_type=f32).astype(bf16).astype(f32)
        for s in range(w // HEAD):
            t = q[:, s * HEAD:(s + 1) * HEAD]
            turned = t * rot_ref[0:1, :] + pltpu.roll(t, HEAD // 2, 1) * rot_ref[1:2, :]
            h = b * (WIDE // HEAD) + s
            qh[h * rows:(h + 1) * rows, :] = turned.astype(bf16).astype(f32)

    pl.semaphore_wait(barrier, 2)

    def attend(it, carry):
        base = pl.multiple_of((it % KV_RING) * (4 * cache), cache)
        whole = kv.at[pl.ds(base, 4 * cache), :]
        pltpu.make_async_copy(whole, whole, kvsem.at[it % KV_RING]).wait()
        row = first_row(it)
        zero = jnp.zeros((8, HEAD), f32)
        for pair in range(KV_ITER // 2):
            ra = row + 2 * pair
            qa = qh[pl.ds(ra, 8, stride=rows), :]
            qb = qh[pl.ds(ra + 1, 8, stride=rows), :]
            q2 = jnp.concatenate(
                [jnp.concatenate([qa, zero], 1), jnp.concatenate([zero, qb], 1)], 0).astype(bf16)
            keys = kv[pl.ds(pl.multiple_of(base + pair * cache, cache), cache), :]
            s = lax.dot_general(q2, keys, (((1,), (1,)), ((), ())), preferred_element_type=f32) * HEAD**-0.5
            e = jnp.exp(s - jnp.max(s, -1, keepdims=True))
            weights = (e * (1.0 / jnp.sum(e, -1, keepdims=True))).astype(bf16)
            values = kv[pl.ds(pl.multiple_of(base + (2 + pair) * cache, cache), cache), :]
            o = jnp.dot(weights, values, preferred_element_type=f32)
            oh[pl.ds(ra, 8, stride=rows), :] = o[0:8, 0:HEAD]
            oh[pl.ds(ra + 1, 8, stride=rows), :] = o[8:16, HEAD:2 * HEAD]

        @pl.when(it + KV_RING < iters)
        def _():
            for c in kv_copies(it + KV_RING):
                c.start()

        @pl.when(jnp.logical_and(it + KV_RING >= iters, it + KV_RING < iters + 3))
        def _():
            for c in pair_copies(it + KV_RING - iters):
                c.start()

        return carry

    def remote(src, dst, send, recv, to):
        return pltpu.make_async_remote_copy(src, dst, send, recv, device_id={axis: to}, device_id_type=MESH)

    def send1l(m):
        return remote(s1l.at[m], r1l.at[m], s1l_s.at[m], s1l_r.at[m], left)

    def send1r(m):
        return remote(s1r.at[m], r1r.at[m], s1r_s.at[m], s1r_r.at[m], right)

    per_chunk = per // KV_ITER
    done = 0
    for ph in phases:
        lax.fori_loop(done * per_chunk, (done + len(ph)) * per_chunk, attend, 0)
        done += len(ph)
        chunks = [owner(distance(i)) for i in ph]
        two = chunks if len(chunks) == 2 else chunks * 2
        lhs = jnp.concatenate(
            [jnp.concatenate([oh[pl.ds(pl.multiple_of(h * rows + c * per, per), per), :] for c in two], 0)
             for h in range(heads)], 1).astype(bf16)
        if ph == phases[0]:
            for t in range(0, wo_blocks, wo_per):
                whole = wbuf.at[6 + t // wo_per, pl.ds(0, min(wo_per, wo_blocks - t) * q_cols), :]
                pltpu.make_async_copy(whole, whole, wsem.at[6 + t // wo_per]).wait()

        def outward(u, carry):
            for v in range(2):
                t = 2 * u + v
                w = wbuf[6 + t // wo_per, pl.ds(pl.multiple_of((t % wo_per) * q_cols, HEAD), q_cols), :]
                term[:, pl.ds(pl.multiple_of(t * WIDE, WIDE), WIDE)] = jnp.dot(lhs, w, preferred_element_type=f32)
            return carry

        lax.fori_loop(0, wo_blocks // 2, outward, 0)
        for a, i in enumerate(ph):
            part = slice(a * per, (a + 1) * per)
            if i == n - 1:
                send1l((n - 2) // 2).wait_recv()
                send1r((n - 2) // 2 - 1).wait_recv()
                for c in range(0, dim, own_cols):
                    cs = slice(c, c + own_cols)
                    h = term[part, cs] + r1l[(n - 2) // 2, :, cs].astype(f32) + r1r[(n - 2) // 2 - 1, :, cs].astype(f32)
                    hbuf[me, :, cs] = (x_ref[me, :, cs].astype(f32) + h).astype(bf16)
            elif i % 2 == 1 or i == 0:
                m = (i + 1) // 2
                if i > 0:
                    send1l(m - 1).wait_recv()
                for c in range(0, dim, own_cols):
                    cs = slice(c, c + own_cols)
                    s = term[part, cs]
                    if i > 0:
                        s = s + r1l[m - 1, :, cs].astype(f32)
                    s1l[m, :, cs] = s.astype(bf16)
                send1l(m).start()
            else:
                m = i // 2 - 1
                if m > 0:
                    send1r(m - 1).wait_recv()
                for c in range(0, dim, own_cols):
                    cs = slice(c, c + own_cols)
                    s = term[part, cs]
                    if m > 0:
                        s = s + r1r[m - 1, :, cs].astype(f32)
                    s1r[m, :, cs] = s.astype(bf16)
                send1r(m).start()

    for p in range(3, SLOTS // 2):
        for c in pair_copies(p):
            c.start()

    hops_r, hops_l = n // 2, n // 2 - 1
    subs = 4
    sub = dim // subs

    def gather1r(hop, s):
        ref = hbuf.at[lax.rem(me + n - hop, n), :, pl.ds(s * sub, sub)]
        return remote(ref, ref, g1r_s.at[hop, s], g1r_r.at[hop, s], right)

    def gather1l(hop, s):
        ref = hbuf.at[lax.rem(me + hop, n), :, pl.ds(s * sub, sub)]
        return remote(ref, ref, g1l_s.at[hop, s], g1l_r.at[hop, s], left)

    for s in range(subs):
        gather1r(0, s).start()
        gather1l(0, s).start()
    for b in range(in_kv):
        down_copy(b).start()
    for hop in range(hops_r):
        for s in range(subs):
            gather1r(hop, s).wait_recv()
            if hop + 1 < hops_r:
                gather1r(hop + 1, s).start()
            if hop < hops_l:
                gather1l(hop, s).wait_recv()
                if hop + 1 < hops_l:
                    gather1l(hop + 1, s).start()

    normed_into(lambda r, c, w: hbuf[r, :, c:c + w].astype(f32), gain_m_ref)

    def expand(p):
        for c in pair_copies(p):
            c.wait()
        slot = 2 * (p % (SLOTS // 2))
        gate = jnp.dot(act[...], wbuf[slot], preferred_element_type=f32)
        up = jnp.dot(act[...], wbuf[slot + 1], preferred_element_type=f32)
        hid[:, pl.ds(pl.multiple_of(p * WIDE, WIDE), WIDE)] = (gate * (1.0 / (1.0 + jnp.exp(-gate))) * up).astype(bf16)

    def expand_first(p, carry):
        expand(p)
        for c in pair_copies(p + SLOTS // 2):
            c.start()
        return carry

    lax.fori_loop(0, pairs - SLOTS // 2, expand_first, 0)
    for p in range(pairs - SLOTS // 2, pairs):
        expand(p)
        at = in_kv + 2 * per_slot * (p - (pairs - SLOTS // 2))
        for b in range(at, at + 2 * per_slot):
            down_copy(b).start()

    def send2l(m, j):
        w = pl.ds(0, widths[j])
        return remote(s2l.at[m, j, :, w], r2l.at[m, j, :, w], s2l_s.at[m, j], s2l_r.at[m, j], left)

    def send2r(m, j):
        w = pl.ds(0, widths[j])
        return remote(s2r.at[m, j, :, w], r2r.at[m, j, :, w], s2r_s.at[m, j], s2r_r.at[m, j], right)

    def gather2r(hop, j):
        ref = ybuf.at[:, pl.ds(column(lax.rem(me + n - hop, n), j), widths[j])]
        return remote(ref, ref, g2r_s.at[hop, j], g2r_r.at[hop, j], right)

    def gather2l(hop, j):
        ref = ybuf.at[:, pl.ds(column(lax.rem(me + hop, n), j), widths[j])]
        return remote(ref, ref, g2l_s.at[hop, j], g2l_r.at[hop, j], left)

    def out_copy(k, j):
        cols = pl.ds(column(lax.rem(me + k, n), j), widths[j])
        return pltpu.make_async_copy(ybuf.at[:, cols], y_ref.at[:, cols], ysem.at[k, j])

    at = 0
    for ph in phases:
        for j, w in enumerate(widths):
            terms = []
            for b in range(at, at + len(ph)):
                down_copy(b).wait()
            for b in range(at, at + len(ph)):
                terms.append(jnp.dot(hid[...], down_place(b)[:, 0:w], preferred_element_type=f32))
            at += len(ph)
            for i, s in zip(ph, terms):
                if i == n - 1:
                    send2l((n - 2) // 2, j).wait_recv()
                    send2r((n - 2) // 2 - 1, j).wait_recv()
                    s = s + r2l[(n - 2) // 2, j, :, 0:w].astype(f32) + r2r[(n - 2) // 2 - 1, j, :, 0:w].astype(f32)
                    cols = pl.ds(column(me, j), w)
                    h = hbuf[:, :, cols].astype(f32).reshape(rows, w)
                    ybuf[:, cols] = (h + s).astype(bf16)
                    gather2r(0, j).start()
                    gather2l(0, j).start()
                    out_copy(0, j).start()
                elif i % 2 == 1 or i == 0:
                    m = (i + 1) // 2
                    if i > 0:
                        send2l(m - 1, j).wait_recv()
                        s = s + r2l[m - 1, j, :, 0:w].astype(f32)
                    s2l[m, j, :, 0:w] = s.astype(bf16)
                    send2l(m, j).start()
                else:
                    m = i // 2 - 1
                    if m > 0:
                        send2r(m - 1, j).wait_recv()
                        s = s + r2r[m - 1, j, :, 0:w].astype(f32)
                    s2r[m, j, :, 0:w] = s.astype(bf16)
                    send2r(m, j).start()

    for hop in range(hops_r):
        for j in range(len(widths)):
            gather2r(hop, j).wait_recv()
            if hop + 1 < hops_r:
                gather2r(hop + 1, j).start()
            out_copy(n - 1 - hop, j).start()
            if hop < hops_l:
                gather2l(hop, j).wait_recv()
                if hop + 1 < hops_l:
                    gather2l(hop + 1, j).start()
                out_copy(hop + 1, j).start()

    for m in range((n - 2) // 2 + 1):
        send1l(m).wait_send()
        for j in range(len(widths)):
            send2l(m, j).wait_send()
    for m in range((n - 2) // 2):
        send1r(m).wait_send()
        for j in range(len(widths)):
            send2r(m, j).wait_send()
    for hop in range(hops_r):
        for s in range(subs):
            gather1r(hop, s).wait_send()
        for j in range(len(widths)):
            gather2r(hop, j).wait_send()
    for hop in range(hops_l):
        for s in range(subs):
            gather1l(hop, s).wait_send()
        for j in range(len(widths)):
            gather2l(hop, j).wait_send()
    for k in range(n):
        for j in range(len(widths)):
            out_copy(k, j).wait()


def solution(mesh):
    n = mesh.shape["tp"]

    def step(x, k_cache, v_cache, gain_a, wq, wo, gain_m, w_gate, w_up, w_down):
        rows, dim = x.shape
        cache = k_cache.shape[1]
        q_cols = wq.shape[1]
        ff = w_gate.shape[1]
        per, own = rows // n, dim // n
        pieces = -(-own // WIDE)
        half = HEAD // 2
        angle = (cache - 1) * float(THETA) ** (-np.arange(half) / half)
        cos, sin = np.cos(angle), np.sin(angle)
        rot = jnp.asarray(np.stack([np.concatenate([cos, cos]), np.concatenate([-sin, sin])]), f32)
        hl, hr = n // 2, n // 2 - 1
        dma = pltpu.SemaphoreType.DMA
        anywhere = pl.BlockSpec(memory_space=pl.ANY)
        inside = pl.BlockSpec(memory_space=pltpu.VMEM)
        return pl.pallas_call(
            functools.partial(kernel, n, "tp"),
            out_shape=jax.ShapeDtypeStruct((rows, dim), bf16),
            in_specs=[inside] * 4 + [anywhere] * 7,
            out_specs=anywhere,
            scratch_shapes=[
                pltpu.VMEM((KV_RING * 4 * cache, WIDE), bf16),
                pltpu.VMEM((SLOTS, dim, WIDE), bf16),
                pltpu.VMEM((rows, dim), bf16),
                pltpu.VMEM((n, per, dim), bf16),
                pltpu.VMEM((rows, dim), bf16),
                pltpu.VMEM((2 * per, dim), f32),
                pltpu.VMEM((rows, ff), bf16),
                pltpu.VMEM((8 * rows, HEAD), f32),
                pltpu.VMEM((8 * rows, HEAD), f32),
                pltpu.VMEM((hl, per, dim), bf16),
                pltpu.VMEM((hr, per, dim), bf16),
                pltpu.VMEM((hl, per, dim), bf16),
                pltpu.VMEM((hr, per, dim), bf16),
                pltpu.VMEM((hl, pieces, rows, WIDE), bf16),
                pltpu.VMEM((hr, pieces, rows, WIDE), bf16),
                pltpu.VMEM((hl, pieces, rows, WIDE), bf16),
                pltpu.VMEM((hr, pieces, rows, WIDE), bf16),
                dma((SLOTS,)),
                dma((KV_RING,)),
                dma((n * pieces,)),
                dma((n, pieces)),
                dma((hl,)), dma((hl,)), dma((hr,)), dma((hr,)),
                dma((hr, 4)), dma((hr, 4)), dma((hl, 4)), dma((hl, 4)),
                dma((hl, pieces)), dma((hl, pieces)), dma((hr, pieces)), dma((hr, pieces)),
                dma((hr, pieces)), dma((hr, pieces)), dma((hl, pieces)), dma((hl, pieces)),
            ],
            compiler_params=pltpu.CompilerParams(
                collective_id=0, has_side_effects=True, vmem_limit_bytes=67043328),
            name="layer",
        )(x.reshape(n, per, dim), rot, gain_a.reshape(1, dim), gain_m.reshape(1, dim),
          k_cache.reshape(rows, cache, HEAD), v_cache.reshape(rows, cache, HEAD), wq, wo, w_gate, w_up, w_down)

    states, cache, columns, rows_of = P("dp", None), P("dp", None, "tp", None), P(None, "tp"), P("tp", None)
    return jax.shard_map(
        step,
        mesh=mesh,
        in_specs=(states, cache, cache, P(None), columns, rows_of, P(None), columns, columns, rows_of),
        out_specs=states,
        check_vma=False,
    )
```

time: 248 us -> 133 us (0.54)
  waiting for transfers between devices: 139 us -> 0 us
  Pallas kernels: 0 us -> 128 us
  matrix products: 87.8 us -> 0 us
  between operations: 13.5 us -> 0.01 us
  other arithmetic: 6.29 us -> 0 us
  local copies, waits for them, and re-layouts: 0.17 us -> 4.82 us
    psum x2 -> x0, waiting for transfers between devices: 139 us -> none  [added(): lax.psum(term.astype(jnp.bfloat16), 'tp').astype(jnp.float32)]
    pallas_call x0 -> x1, Pallas kernels: none -> 128 us  [step(): pl.pallas_call(functools.partial(kernel, n, 'tp'), out_shape=jax.ShapeDty...]
    dot_general x5 -> x0, matrix products: 70.9 us -> none  [the longest x1 26.6 us: step(): jnp.dot(hidden_of(normed(h, gain_m), w_gate, w_up), w_down, preferred_ele...]
    sub x1 -> x0, matrix products: 16.9 us -> none  [seen_by(): weights = jax.nn.softmax(scores, -1).astype(jnp.bfloat16)]
    reduce_sum x2 -> x0, other arithmetic: 3.06 us -> none  [normed(): scale = lax.rsqrt(jnp.mean(wide * wide, -1, keepdims=True) + 1e-06)]
    convert_element_type x3 -> x0, other arithmetic: 3.04 us -> none  [the longest x1 2.31 us: added(): (t.astype(jnp.float32) + lax.psum(term.astype(jnp.bfloat16), 'tp').astype...]
    reshape x1 -> x2, local copies, waits for them, and re-layouts: 0.15 us -> 2.66 us  [the longest x1 1.34 us: step(): gain_a.reshape(1, dim)]
  transfers between devices with their start and end apart: 2 -> 0, of which waited for: 2 -> 0; matrix products, arithmetic and copies ran while one was open for 0% -> 0% of each run, Pallas kernels for 0% -> 0%
where the time goes in v1:
time: 133 us; the launch traced here: 132 us
  Pallas kernels  128 us (96%)
  local copies, waits for them, and re-layouts  4.82 us (4%)
    pallas_call x1, Pallas kernels, step(): pl.pallas_call(functools.partial(kernel, n, 'tp'), out_shape=jax.ShapeDty...  128 us

profile of v1, /device:TPU:30, one launch (start us, length us, event | category | flops | bytes accessed | tf_op | source)
XLA Modules:
  0.0 132.3 jit_solution(16841278826876095157)
XLA Ops:
  0.0 1.3 %reshape.16.gain_a_ref = bf16[1,7168]{1,0:T(2,128)(2,1)} reshape(bf16[7168]{0:T(1024)(128)(2,1)} %param.14) | data formatting | bytes 28672 | tf_op jit(solution)/shard_map/reshape | solution.py:438
  1.3 1.3 %reshape.17.gain_m_ref = bf16[1,7168]{1,0:T(2,128)(2,1)} reshape(bf16[7168]{0:T(1024)(128)(2,1)} %param.17) | data formatting | bytes 28672 | tf_op jit(solution)/shard_map/reshape | solution.py:438
  2.7 127.5 %layer.1 = bf16[64,7168]{1,0:T(8,128)(2,1)} custom-call(bf16[8,8,7168]{2,1,0:T(8,128)(2,1)} %bitcast.5, f32[2,128]{1,0:T(2,128)} %constant.2.clone.rot_ref, bf16[1,7168]{1,0:T(2,128)(2,1)} %reshape.16.gain_a_ref, bf16[1,7168]{1,0:T(2,128)(2,1)} %reshape.17.gain_m_ref, bf16[64,2048,128]{2,1,0:T(8,128)(2,1)} %bitcast.3, bf16[64,2048,128]{2,1,0:T(8,128)(2,1)} %bitcast.4, ...), custom_call_target="tpu_custom_call" | custom-call | tf_op jit(solution)/shard_map/layer/pallas_call | solution.py:403
  130.2 2.2 %copy.13 = bf16[64,7168]{1,0:T(8,128)(2,1)} copy(bf16[64,7168]{1,0:T(8,128)(2,1)} %layer.1) | data formatting | bytes 1835008

commit v2 on v1

v2 whole, which is shorter than its diff:
```python
import functools

import jax
import jax.numpy as jnp
import numpy as np
from jax import lax
from jax.experimental import pallas as pl
from jax.experimental.pallas import tpu as pltpu
from jax.sharding import PartitionSpec as P

HEAD = 128
THETA = 10000
MESH = pl.DeviceIdType.MESH
WIDE = 256
SLOTS = 8
KV_ITER = 4
KV_RING = 6

bf16, f32 = jnp.bfloat16, jnp.float32


def distance(k):
    odd = k % 2
    return 4 + odd * ((k + 1) // 2) - (1 - odd) * (k // 2)


def kernel(n, axis, x_ref, rot_ref, gain_a_ref, gain_m_ref, k_ref, v_ref, wq_ref, wo_ref, wg_ref, wu_ref, wd_ref, y_ref,
           kv, wbuf, act, hbuf, ybuf, term, hid, qh, oh, sa, sb, tbuf,
           s1l, s1r, r1l, r1r, s2l, s2r, r2l, r2r,
           wsem, ksem, vsem, dsem, ysem,
           s1l_s, s1l_r, s1r_s, s1r_r, g1l_s, g1l_r, g1r_s, g1r_r,
           s2l_s, s2l_r, s2r_s, s2r_r, g2l_s, g2l_r, g2r_s, g2r_r):
    me = lax.axis_index(axis)
    right, left = lax.rem(me + 1, n), lax.rem(me + n - 1, n)
    rows, dim = act.shape
    per = rows // n
    cache = k_ref.shape[1]
    q_cols = wq_ref.shape[1]
    heads = q_cols // HEAD
    ff = wg_ref.shape[1]
    own_cols = dim // n
    widths = [min(WIDE, own_cols - j) for j in range(0, own_cols, WIDE)]
    pairs = ff // WIDE
    iters = rows // KV_ITER
    wo_per = wbuf.shape[1] // q_cols
    wo_blocks = dim // WIDE
    wo_slot = SLOTS // 2
    hl, hr = n // 2, n // 2 - 1
    v_base = KV_RING * 2 * cache

    def owner(k):
        return lax.rem(me + k, n)

    barrier = pltpu.get_barrier_semaphore()
    for other in (left, right):
        pl.semaphore_signal(barrier, inc=1, device_id={axis: other}, device_id_type=MESH)

    def wq_copy(b):
        w = min(WIDE, q_cols - b * WIDE)
        return pltpu.make_async_copy(wq_ref.at[:, pl.ds(b * WIDE, w)], wbuf.at[b, :, pl.ds(0, w)], wsem.at[b])

    q_blocks = -(-q_cols // WIDE)

    def wo_copy(t):
        return pltpu.make_async_copy(
            wo_ref.at[:, pl.ds(t * WIDE, WIDE)],
            wbuf.at[wo_slot + t // wo_per, pl.ds((t % wo_per) * q_cols, q_cols), :],
            wsem.at[wo_slot + t // wo_per])

    def first_row(it):
        return owner(distance(it // 2)) * per + (it % 2) * KV_ITER

    def slot_row(it, base):
        return pl.multiple_of(base + (it % KV_RING) * (2 * cache), cache)

    def cache_start(it, ref, base, sem):
        for s in range(KV_ITER):
            pltpu.make_async_copy(
                ref.at[first_row(it) + s],
                kv.at[pl.ds(slot_row(it, base) + (s // 2) * cache, cache), pl.ds((s % 2) * HEAD, HEAD)],
                sem.at[it % KV_RING]).start()

    def cache_wait(it, base, sem):
        whole = kv.at[pl.ds(slot_row(it, base), 2 * cache), :]
        pltpu.make_async_copy(whole, whole, sem.at[it % KV_RING]).wait()

    def k_start(it):
        cache_start(it, k_ref, 0, ksem)

    def v_start(it):
        cache_start(it, v_ref, v_base, vsem)

    def pair_copies(p):
        cols = pl.ds(pl.multiple_of(p * WIDE, WIDE), WIDE)
        slot = 2 * (p % (SLOTS // 2))
        return (pltpu.make_async_copy(wg_ref.at[:, cols], wbuf.at[slot], wsem.at[slot]),
                pltpu.make_async_copy(wu_ref.at[:, cols], wbuf.at[slot + 1], wsem.at[slot + 1]))

    def pair_start(p):
        for c in pair_copies(p):
            c.start()

    phases = [(0,)] + [(i, i + 1) for i in range(1, n - 1, 2)] + [(n - 1,)]
    order = [(i, j) for ph in phases for j in range(len(widths)) for i in ph]
    in_kv = kv.shape[0] // ff
    per_slot = wbuf.shape[1] // ff

    def down_place(b):
        if b < in_kv:
            return kv.at[pl.ds(b * ff, ff), :]
        b -= in_kv
        return wbuf.at[(2 * pairs + b // per_slot) % SLOTS, pl.ds((b % per_slot) * ff, ff), :]

    def column(o, j):
        return pl.multiple_of(o * own_cols + j * WIDE, HEAD)

    def down_copy(b):
        i, j = order[b]
        w = widths[j]
        return pltpu.make_async_copy(
            wd_ref.at[:, pl.ds(column(owner(distance(i)), j), w)], down_place(b).at[:, pl.ds(0, w)], dsem.at[b])

    for b in range(q_blocks):
        wq_copy(b).start()

    def normed_into(read, gain_ref):
        def group(g, carry):
            def wide(l):
                return jnp.concatenate([read(2 * g, l), read(2 * g + 1, l)], 0)

            total = [jnp.zeros((2 * per, HEAD), f32) for _ in range(4)]
            for l in range(dim // HEAD):
                t = wide(l)
                total[l % 4] = total[l % 4] + t * t
            total = (total[0] + total[1]) + (total[2] + total[3])
            scale = lax.rsqrt(jnp.sum(total, -1, keepdims=True) / dim + 1e-6)
            r = pl.ds(pl.multiple_of(g * 2 * per, 2 * per), 2 * per)
            for l in range(dim // HEAD):
                act[r, l * HEAD:(l + 1) * HEAD] = (wide(l) * scale * gain_ref[l:l + 1, :].astype(f32)).astype(bf16)
            return carry

        lax.fori_loop(0, n // 2, group, 0)

    normed_into(lambda r, l: x_ref[r, :, l * HEAD:(l + 1) * HEAD].astype(f32), gain_a_ref)

    r1l[0] = jnp.zeros(r1l.shape[1:], bf16)
    r1r[0] = jnp.zeros(r1r.shape[1:], bf16)
    started = 0
    for b in range(0, q_blocks, 2):
        both = range(b, min(b + 2, q_blocks))
        for c in both:
            wq_copy(c).wait()
        if b == 0:
            for it in range(KV_RING):
                k_start(it)
                v_start(it)
            for t in range(wo_blocks):
                wo_copy(t).start()
        dots = [jnp.dot(act[...], wbuf[c, :, :min(WIDE, q_cols - c * WIDE)], preferred_element_type=f32) for c in both]
        for c, q in zip(both, dots):
            q = q.astype(bf16).astype(f32)
            for s in range(q.shape[1] // HEAD):
                t = q[:, s * HEAD:(s + 1) * HEAD]
                turned = t * rot_ref[0:1, :] + pltpu.roll(t, HEAD // 2, 1) * rot_ref[1:2, :]
                h = c * (WIDE // HEAD) + s
                qh[h * rows:(h + 1) * rows, :] = turned.astype(bf16).astype(f32)
    qh[heads * rows:, :] = jnp.zeros((qh.shape[0] - heads * rows, HEAD), f32)
    pl.semaphore_wait(barrier, 2)

    def scores(it, s_ref):
        row = first_row(it)
        zero = jnp.zeros((8, HEAD), f32)
        for pair in range(KV_ITER // 2):
            ra = row + 2 * pair
            qa = qh[pl.ds(ra, 8, stride=rows), :]
            qb = qh[pl.ds(ra + 1, 8, stride=rows), :]
            q2 = jnp.concatenate(
                [jnp.concatenate([qa, zero], 1), jnp.concatenate([zero, qb], 1)], 0).astype(bf16)
            keys = kv[pl.ds(slot_row(it, 0) + pair * cache, cache), :]
            s_ref[pair * 16:(pair + 1) * 16, :] = lax.dot_general(
                q2, keys, (((1,), (1,)), ((), ())), preferred_element_type=f32)

    def finish(it, s_ref):
        row = first_row(it)
        for pair in range(KV_ITER // 2):
            ra = row + 2 * pair
            s = s_ref[pair * 16:(pair + 1) * 16, :] * HEAD**-0.5
            e = jnp.exp(s - jnp.max(s, -1, keepdims=True))
            weights = (e * (1.0 / jnp.sum(e, -1, keepdims=True))).astype(bf16)
            values = kv[pl.ds(slot_row(it, v_base) + pair * cache, cache), :]
            o = jnp.dot(weights, values, preferred_element_type=f32)
            oh[pl.ds(ra, 8, stride=rows), :] = o[0:8, 0:HEAD]
            oh[pl.ds(ra + 1, 8, stride=rows), :] = o[8:16, HEAD:2 * HEAD]

    def attend(k, carry):
        cache_wait(2 * k, v_base, vsem)
        cache_wait(2 * k + 1, v_base, vsem)
        cache_wait(2 * k + 1, 0, ksem)

        @pl.when(k < n - 1)
        def _():
            cache_wait(2 * k + 2, 0, ksem)

        scores(2 * k + 1, sb)
        finish(2 * k, sa)
        scores(2 * k + 2, sa)
        finish(2 * k + 1, sb)

        @pl.when(2 * k + 1 + KV_RING < iters)
        def _():
            k_start(2 * k + 1 + KV_RING)
            v_start(2 * k + KV_RING)
            v_start(2 * k + 1 + KV_RING)

        @pl.when(2 * k + 2 + KV_RING < iters)
        def _():
            k_start(2 * k + 2 + KV_RING)

        @pl.when(jnp.logical_and(k >= n - 3, k < n - 1))
        def _():
            pair_start(k - (n - 3))

        return carry

    def remote(src, dst, send, recv, to):
        return pltpu.make_async_remote_copy(src, dst, send, recv, device_id={axis: to}, device_id_type=MESH)

    def send1l(m):
        return remote(s1l.at[m], r1l.at[m + 1], s1l_s.at[m], s1l_r.at[m], left)

    def send1r(m):
        return remote(s1r.at[m], r1r.at[m + 1], s1r_s.at[m], s1r_r.at[m], right)

    strips = [slice(c, c + own_cols) for c in range(0, dim, own_cols)]
    body = wo_blocks // 2

    def phase(p, carry):
        lax.fori_loop(jnp.maximum(0, 2 * p - 1), jnp.minimum(n, 2 * p + 1), attend, 0)

        @pl.when(p == 0)
        def _():
            for t in range(0, wo_blocks, wo_per):
                whole = wbuf.at[wo_slot + t // wo_per, pl.ds(0, min(wo_per, wo_blocks - t) * q_cols), :]
                pltpu.make_async_copy(whole, whole, wsem.at[wo_slot + t // wo_per]).wait()

        two = [owner(distance(jnp.maximum(0, 2 * p - 1))), owner(distance(jnp.minimum(n - 1, 2 * p)))]
        lhs = jnp.concatenate(
            [jnp.concatenate([oh[pl.ds(pl.multiple_of(h * rows + c * per, per), per), :] for c in two], 0)
             for h in range(heads)], 1).astype(bf16)

        def outward(u, carry):
            for v in range(body):
                t = u * body + v
                w = wbuf[wo_slot + t // wo_per, pl.ds(pl.multiple_of((t % wo_per) * q_cols, HEAD), q_cols), :]
                term[:, pl.ds(pl.multiple_of(t * WIDE, WIDE), WIDE)] = jnp.dot(lhs, w, preferred_element_type=f32)
            return carry

        lax.fori_loop(0, wo_blocks // body, outward, 0)

        @pl.when(jnp.logical_and(p > 0, p < hl))
        def _():
            send1l(p - 1).wait_recv()

        @pl.when(p < hl)
        def _():
            for cs in strips:
                s1l[p, :, cs] = (term[0:per, cs] + r1l[p, :, cs].astype(f32)).astype(bf16)
            send1l(p).start()

        @pl.when(jnp.logical_and(p > 1, p < hl))
        def _():
            send1r(p - 2).wait_recv()

        @pl.when(jnp.logical_and(p > 0, p < hl))
        def _():
            for cs in strips:
                s1r[p - 1, :, cs] = (term[per:2 * per, cs] + r1r[p - 1, :, cs].astype(f32)).astype(bf16)
            send1r(p - 1).start()

        return carry

    cache_wait(0, 0, ksem)
    scores(0, sa)
    k_start(KV_RING)
    lax.fori_loop(0, hl + 1, phase, 0)

    for p in range(2, SLOTS // 2):
        pair_start(p)

    send1l(hl - 1).wait_recv()
    send1r(hr - 1).wait_recv()
    for cs in strips:
        s = term[0:per, cs] + r1l[hl, :, cs].astype(f32) + r1r[hr, :, cs].astype(f32)
        hbuf[me, :, cs] = (x_ref[me, :, cs].astype(f32) + s).astype(bf16)

    subs = 4
    sub = dim // subs

    def gather1r(hop, s):
        ref = hbuf.at[lax.rem(me + n - hop, n), :, pl.ds(s * sub, sub)]
        return remote(ref, ref, g1r_s.at[hop, s], g1r_r.at[hop, s], right)

    def gather1l(hop, s):
        ref = hbuf.at[lax.rem(me + hop, n), :, pl.ds(s * sub, sub)]
        return remote(ref, ref, g1l_s.at[hop, s], g1l_r.at[hop, s], left)

    for s in range(subs):
        gather1r(0, s).start()
        gather1l(0, s).start()
    for b in range(in_kv):
        down_copy(b).start()
    for hop in range(hl):
        for s in range(subs):
            gather1r(hop, s).wait_recv()
            if hop + 1 < hl:
                gather1r(hop + 1, s).start()
            if hop < hr:
                gather1l(hop, s).wait_recv()
                if hop + 1 < hr:
                    gather1l(hop + 1, s).start()

    normed_into(lambda r, l: hbuf[r, :, l * HEAD:(l + 1) * HEAD].astype(f32), gain_m_ref)

    def expand(p, carry):
        for c in pair_copies(p):
            c.wait()
        slot = 2 * (p % (SLOTS // 2))
        gate = jnp.dot(act[...], wbuf[slot], preferred_element_type=f32)
        up = jnp.dot(act[...], wbuf[slot + 1], preferred_element_type=f32)
        hid[:, pl.ds(pl.multiple_of(p * WIDE, WIDE), WIDE)] = (gate * (1.0 / (1.0 + jnp.exp(-gate))) * up).astype(bf16)

        @pl.when(p + SLOTS // 2 < pairs)
        def _():
            pair_start(p + SLOTS // 2)

        for late in range(pairs - SLOTS // 2, pairs):
            @pl.when(p == late)
            def _():
                at = in_kv + 2 * per_slot * (late - (pairs - SLOTS // 2))
                for b in range(at, min(at + 2 * per_slot, len(order))):
                    down_copy(b).start()

        return carry

    lax.fori_loop(0, pairs, expand, 0)

    def send2l(m, j):
        w = pl.ds(0, widths[j])
        return remote(s2l.at[m, j, :, w], r2l.at[m, j, :, w], s2l_s.at[m, j], s2l_r.at[m, j], left)

    def send2r(m, j):
        w = pl.ds(0, widths[j])
        return remote(s2r.at[m, j, :, w], r2r.at[m, j, :, w], s2r_s.at[m, j], s2r_r.at[m, j], right)

    def gather2r(hop, j):
        ref = ybuf.at[:, pl.ds(column(lax.rem(me + n - hop, n), j), widths[j])]
        return remote(ref, ref, g2r_s.at[hop, j], g2r_r.at[hop, j], right)

    def gather2l(hop, j):
        ref = ybuf.at[:, pl.ds(column(lax.rem(me + hop, n), j), widths[j])]
        return remote(ref, ref, g2l_s.at[hop, j], g2l_r.at[hop, j], left)

    def out_copy(k, j):
        cols = pl.ds(column(lax.rem(me + k, n), j), widths[j])
        return pltpu.make_async_copy(ybuf.at[:, cols], y_ref.at[:, cols], ysem.at[k, j])

    def place(i):
        return ("l", (i + 1) // 2) if i % 2 == 1 or i == 0 else ("r", i // 2 - 1)

    steps, at = [], 0
    for ph in phases:
        for j in range(len(widths)):
            steps.append((ph, j, list(range(at, at + len(ph)))))
            at += len(ph)
    for t in range(len(steps) + 1):
        now = steps[t] if t < len(steps) else None
        last = steps[t - 1] if t > 0 else None
        if now:
            for b in now[2]:
                down_copy(b).wait()
        if last:
            j = last[1]
            for i in last[0]:
                if i == n - 1:
                    send2l(hl - 1, j).wait_recv()
                    send2r(hr - 1, j).wait_recv()
                else:
                    side, m = place(i)
                    if m > 0:
                        (send2l if side == "l" else send2r)(m - 1, j).wait_recv()
        terms = []
        if now:
            w = widths[now[1]]
            for b in now[2]:
                if len(now[2]) == 2:
                    terms.append(jnp.dot(hid[...], down_place(b)[:, 0:w], preferred_element_type=f32))
                else:
                    terms.append(jnp.dot(hid[:, :ff // 2], down_place(b)[:ff // 2, 0:w], preferred_element_type=f32)
                                 + jnp.dot(hid[:, ff // 2:], down_place(b)[ff // 2:, 0:w], preferred_element_type=f32))
        if last:
            j, w = last[1], widths[last[1]]
            for a, i in enumerate(last[0]):
                s = tbuf[(t - 1) % 2, a, :, 0:w]
                if i == n - 1:
                    s = s + r2l[hl - 1, j, :, 0:w].astype(f32) + r2r[hr - 1, j, :, 0:w].astype(f32)
                    cols = pl.ds(column(me, j), w)
                    ybuf[:, cols] = (hbuf[:, :, cols].astype(f32).reshape(rows, w) + s).astype(bf16)
                else:
                    side, m = place(i)
                    src, got = (s2l, r2l) if side == "l" else (s2r, r2r)
                    if m > 0:
                        s = s + got[m - 1, j, :, 0:w].astype(f32)
                    src[m, j, :, 0:w] = s.astype(bf16)
        for a, s in enumerate(terms):
            tbuf[t % 2, a, :, 0:widths[now[1]]] = s
        if last:
            for i in last[0]:
                if i == n - 1:
                    gather2r(0, j).start()
                    gather2l(0, j).start()
                    out_copy(0, j).start()
                else:
                    side, m = place(i)
                    (send2l if side == "l" else send2r)(m, j).start()

    for hop in range(hl):
        for j in range(len(widths)):
            gather2r(hop, j).wait_recv()
            if hop + 1 < hl:
                gather2r(hop + 1, j).start()
            out_copy(n - 1 - hop, j).start()
            if hop < hr:
                gather2l(hop, j).wait_recv()
                if hop + 1 < hr:
                    gather2l(hop + 1, j).start()
                out_copy(hop + 1, j).start()

    for m in range(hl):
        send1l(m).wait_send()
        for j in range(len(widths)):
            send2l(m, j).wait_send()
    for m in range(hr):
        send1r(m).wait_send()
        for j in range(len(widths)):
            send2r(m, j).wait_send()
    for hop in range(hl):
        for s in range(subs):
            gather1r(hop, s).wait_send()
        for j in range(len(widths)):
            gather2r(hop, j).wait_send()
    for hop in range(hr):
        for s in range(subs):
            gather1l(hop, s).wait_send()
        for j in range(len(widths)):
            gather2l(hop, j).wait_send()
    for k in range(n):
        for j in range(len(widths)):
            out_copy(k, j).wait()


def solution(mesh):
    n = mesh.shape["tp"]

    def step(x, k_cache, v_cache, gain_a, wq, wo, gain_m, w_gate, w_up, w_down):
        rows, dim = x.shape
        cache = k_cache.shape[1]
        q_cols = wq.shape[1]
        ff = w_gate.shape[1]
        per, own = rows // n, dim // n
        pieces = -(-own // WIDE)
        half = HEAD // 2
        angle = (cache - 1) * float(THETA) ** (-np.arange(half) / half)
        cos, sin = np.cos(angle), np.sin(angle)
        rot = jnp.asarray(np.stack([np.concatenate([cos, cos]), np.concatenate([-sin, sin])]), f32)
        hl, hr = n // 2, n // 2 - 1
        dma = pltpu.SemaphoreType.DMA
        anywhere = pl.BlockSpec(memory_space=pl.ANY)
        inside = pl.BlockSpec(memory_space=pltpu.VMEM)
        return pl.pallas_call(
            functools.partial(kernel, n, "tp"),
            out_shape=jax.ShapeDtypeStruct((rows, dim), bf16),
            in_specs=[inside] * 4 + [anywhere] * 7,
            out_specs=anywhere,
            scratch_shapes=[
                pltpu.VMEM((KV_RING * 4 * cache, WIDE), bf16),
                pltpu.VMEM((SLOTS, dim, WIDE), bf16),
                pltpu.VMEM((rows, dim), bf16),
                pltpu.VMEM((n, per, dim), bf16),
                pltpu.VMEM((rows, dim), bf16),
                pltpu.VMEM((2 * per, dim), f32),
                pltpu.VMEM((rows, ff), bf16),
                pltpu.VMEM((8 * rows, HEAD), f32),
                pltpu.VMEM((8 * rows, HEAD), f32),
                pltpu.VMEM((8 * KV_ITER, cache), f32),
                pltpu.VMEM((8 * KV_ITER, cache), f32),
                pltpu.VMEM((2, 2, rows, WIDE), f32),
                pltpu.VMEM((hl, per, dim), bf16),
                pltpu.VMEM((hr, per, dim), bf16),
                pltpu.VMEM((hl + 1, per, dim), bf16),
                pltpu.VMEM((hr + 1, per, dim), bf16),
                pltpu.VMEM((hl, pieces, rows, WIDE), bf16),
                pltpu.VMEM((hr, pieces, rows, WIDE), bf16),
                pltpu.VMEM((hl, pieces, rows, WIDE), bf16),
                pltpu.VMEM((hr, pieces, rows, WIDE), bf16),
                dma((SLOTS,)),
                dma((KV_RING,)),
                dma((KV_RING,)),
                dma((n * pieces,)),
                dma((n, pieces)),
                dma((hl,)), dma((hl,)), dma((hr,)), dma((hr,)),
                dma((hr, 4)), dma((hr, 4)), dma((hl, 4)), dma((hl, 4)),
                dma((hl, pieces)), dma((hl, pieces)), dma((hr, pieces)), dma((hr, pieces)),
                dma((hr, pieces)), dma((hr, pieces)), dma((hl, pieces)), dma((hl, pieces)),
            ],
            compiler_params=pltpu.CompilerParams(
                collective_id=0, has_side_effects=True, vmem_limit_bytes=67043328),
            name="layer",
        )(x.reshape(n, per, dim), rot, gain_a.reshape(dim // HEAD, HEAD), gain_m.reshape(dim // HEAD, HEAD),
          k_cache.reshape(rows, cache, HEAD), v_cache.reshape(rows, cache, HEAD), wq, wo, w_gate, w_up, w_down)

    states, cache, columns, rows_of = P("dp", None), P("dp", None, "tp", None), P(None, "tp"), P("tp", None)
    return jax.shard_map(
        step,
        mesh=mesh,
        in_specs=(states, cache, cache, P(None), columns, rows_of, P(None), columns, columns, rows_of),
        out_specs=states,
        check_vma=False,
    )
```

time: 133 us -> 114 us (0.86)
  Pallas kernels: 128 us -> 112 us
  local copies, waits for them, and re-layouts: 4.82 us -> 2.16 us
    pallas_call x1, Pallas kernels: 128 us -> 112 us  [step(): pl.pallas_call(functools.partial(kernel, n, 'tp'), out_shape=jax.ShapeDty...]
    reshape x2 -> x0, local copies, waits for them, and re-layouts: 2.66 us -> none  [the longest x1 1.34 us: step(): gain_a.reshape(1, dim)]
where the time goes in v2:
time: 114 us
  Pallas kernels  112 us (98%)
  local copies, waits for them, and re-layouts  2.16 us (2%)
    pallas_call x1, Pallas kernels, step(): pl.pallas_call(functools.partial(kernel, n, 'tp'), out_shape=jax.ShapeDty...  112 us

profile of v2, /device:TPU:30, one launch (start us, length us, event | category | flops | bytes accessed | tf_op | source)
XLA Modules:
  0.0 114.1 jit_solution(7522069768999120126)
XLA Ops:
  0.0 111.9 %layer.1 = bf16[64,7168]{1,0:T(8,128)(2,1)} custom-call(bf16[8,8,7168]{2,1,0:T(8,128)(2,1)} %bitcast.7, f32[2,128]{1,0:T(2,128)} %constant.2.clone.rot_ref, bf16[56,128]{1,0:T(8,128)(2,1)} %bitcast.8, bf16[56,128]{1,0:T(8,128)(2,1)} %bitcast.9, bf16[64,2048,128]{2,1,0:T(8,128)(2,1)} %bitcast.5, bf16[64,2048,128]{2,1,0:T(8,128)(2,1)} %bitcast.6, ...), custom_call_target="tpu_custom_call" | custom-call | tf_op jit(solution)/shard_map/layer/pallas_call | solution.py:479
  111.9 2.2 %copy.13 = bf16[64,7168]{1,0:T(8,128)(2,1)} copy(bf16[64,7168]{1,0:T(8,128)(2,1)} %layer.1) | data formatting | bytes 1835008

commit v3 on v2

--- a/solution.py
+++ b/solution.py
@@ -26,10 +26,10 @@
 
 def kernel(n, axis, x_ref, rot_ref, gain_a_ref, gain_m_ref, k_ref, v_ref, wq_ref, wo_ref, wg_ref, wu_ref, wd_ref, y_ref,
            kv, wbuf, act, hbuf, ybuf, term, hid, qh, oh, sa, sb, tbuf,
-           s1l, s1r, r1l, r1r, s2l, s2r, r2l, r2r,
-           wsem, ksem, vsem, dsem, ysem,
+           s1l, s1r, r1l, r1r, s2, r2,
+           wsem, gsem, ksem, vsem, dsem, ysem,
            s1l_s, s1l_r, s1r_s, s1r_r, g1l_s, g1l_r, g1r_s, g1r_r,
-           s2l_s, s2l_r, s2r_s, s2r_r, g2l_s, g2l_r, g2r_s, g2r_r):
+           s2_s, s2_r, g3_s, g3_r, g2l_s, g2l_r, g2r_s, g2r_r):
     me = lax.axis_index(axis)
     right, left = lax.rem(me + 1, n), lax.rem(me + n - 1, n)
     rows, dim = act.shape
@@ -52,7 +52,7 @@
         return lax.rem(me + k, n)
 
     barrier = pltpu.get_barrier_semaphore()
-    for other in (left, right):
+    for other in (left, right, lax.rem(me + 2, n), lax.rem(me + n - 2, n)):
         pl.semaphore_signal(barrier, inc=1, device_id={axis: other}, device_id_type=MESH)
 
     def wq_copy(b):
@@ -90,35 +90,73 @@
     def v_start(it):
         cache_start(it, v_ref, v_base, vsem)
 
-    def pair_copies(p):
+    in_wbuf = SLOTS // 2
+    in_kv = kv.shape[0] // (2 * dim)
+    segments = (0, in_wbuf, in_wbuf + in_kv, pairs)
+
+    def pair_ref(seg, q, which):
+        if seg == 1:
+            return kv.at[pl.ds(pl.multiple_of((2 * q + which) * dim, dim), dim), :]
+        return wbuf.at[2 * q + which]
+
+    def pair_copies(seg, q):
+        p = segments[seg] + q
         cols = pl.ds(pl.multiple_of(p * WIDE, WIDE), WIDE)
-        slot = 2 * (p % (SLOTS // 2))
-        return (pltpu.make_async_copy(wg_ref.at[:, cols], wbuf.at[slot], wsem.at[slot]),
-                pltpu.make_async_copy(wu_ref.at[:, cols], wbuf.at[slot + 1], wsem.at[slot + 1]))
-
-    def pair_start(p):
-        for c in pair_copies(p):
+        return [pltpu.make_async_copy(ref.at[:, cols], pair_ref(seg, q, which), gsem.at[2 * p + which])
+                for which, ref in enumerate((wg_ref, wu_ref))]
+
+    def pair_start(seg, q):
+        for c in pair_copies(seg, q):
             c.start()
 
-    phases = [(0,)] + [(i, i + 1) for i in range(1, n - 1, 2)] + [(n - 1,)]
-    order = [(i, j) for ph in phases for j in range(len(widths)) for i in ph]
-    in_kv = kv.shape[0] // ff
-    per_slot = wbuf.shape[1] // ff
-
-    def down_place(b):
-        if b < in_kv:
-            return kv.at[pl.ds(b * ff, ff), :]
-        b -= in_kv
-        return wbuf.at[(2 * pairs + b // per_slot) % SLOTS, pl.ds((b % per_slot) * ff, ff), :]
+    halves = ((0, 1), (2, 3))
+    turn = (1, -1)
+    far, near3, other3, near1, other1, near2, other2, own = range(8)
+    owner_at = (4, -3, 3, -1, 1, -2, 2, 0)
+    target_at = (-2, -1, 1, -1, 1, -2, 2)
+    needs = {near2: (far, near3), other2: (other3,), own: (near1, other1, near2, other2)}
+    steps = [(0, far), (0, near3), (0, other3), (1, far), (1, near3), (1, other3), (0, near1), (0, other1),
+             (0, near2), (0, other2), (1, near1), (1, other1), (0, own), (1, near2), (1, other2), (1, own)]
+    order = [(half, role, j) for half, role in steps for j in halves[half]]
+
+    def at(shift):
+        return lax.rem(me + shift % n, n)
+
+    tail = 2 * in_kv * dim
+    tail_blocks = (kv.shape[0] - tail) // ff
+    slot_blocks = dim // ff
+    kv_blocks = 2 * dim // ff
+    places, after = [], {}
+    for b in range(tail_blocks):
+        places.append(kv.at[pl.ds(tail + b * ff, ff), :])
+    after[None] = range(len(places))
+
+    def free_wbuf(key, slot):
+        first = len(places)
+        for c in range(2 * slot_blocks):
+            places.append(wbuf.at[slot + c // slot_blocks, pl.ds((c % slot_blocks) * ff, ff), :])
+        after[key] = range(min(first, len(order)), min(len(places), len(order)))
+
+    again = segments[3] - segments[2]
+    for q in range(again, in_wbuf):
+        free_wbuf((0, q), 2 * q)
+    for q in range(in_kv):
+        first = len(places)
+        for c in range(kv_blocks):
+            places.append(kv.at[pl.ds(2 * q * dim + c * ff, ff), :])
+        after[(1, q)] = range(min(first, len(order)), min(len(places), len(order)))
+    for q in range(again):
+        free_wbuf((2, q), 2 * q)
 
     def column(o, j):
         return pl.multiple_of(o * own_cols + j * WIDE, HEAD)
 
     def down_copy(b):
-        i, j = order[b]
+        half, role, j = order[b]
         w = widths[j]
         return pltpu.make_async_copy(
-            wd_ref.at[:, pl.ds(column(owner(distance(i)), j), w)], down_place(b).at[:, pl.ds(0, w)], dsem.at[b])
+            wd_ref.at[:, pl.ds(column(at(turn[half] * owner_at[role]), j), w)],
+            places[b].at[:, pl.ds(0, w)], dsem.at[b])
 
     for b in range(q_blocks):
         wq_copy(b).start()
@@ -165,7 +203,7 @@
                 h = c * (WIDE // HEAD) + s
                 qh[h * rows:(h + 1) * rows, :] = turned.astype(bf16).astype(f32)
     qh[heads * rows:, :] = jnp.zeros((qh.shape[0] - heads * rows, HEAD), f32)
-    pl.semaphore_wait(barrier, 2)
+    pl.semaphore_wait(barrier, 4)
 
     def scores(it, s_ref):
         row = first_row(it)
@@ -216,9 +254,10 @@
         def _():
             k_start(2 * k + 2 + KV_RING)
 
-        @pl.when(jnp.logical_and(k >= n - 3, k < n - 1))
-        def _():
-            pair_start(k - (n - 3))
+        for q in range(2):
+            @pl.when(k == n - 3 + q)
+            def _():
+                pair_start(0, q)
 
         return carry
 
@@ -284,8 +323,10 @@
     k_start(KV_RING)
     lax.fori_loop(0, hl + 1, phase, 0)
 
-    for p in range(2, SLOTS // 2):
-        pair_start(p)
+    for q in range(2, in_wbuf):
+        pair_start(0, q)
+    for q in range(in_kv):
+        pair_start(1, q)
 
     send1l(hl - 1).wait_recv()
     send1r(hr - 1).wait_recv()
@@ -307,7 +348,7 @@
     for s in range(subs):
         gather1r(0, s).start()
         gather1l(0, s).start()
-    for b in range(in_kv):
+    for b in after[None]:
         down_copy(b).start()
     for hop in range(hl):
         for s in range(subs):
@@ -321,138 +362,159 @@
 
     normed_into(lambda r, l: hbuf[r, :, l * HEAD:(l + 1) * HEAD].astype(f32), gain_m_ref)
 
-    def expand(p, carry):
-        for c in pair_copies(p):
+    def expand(seg, q, carry):
+        for c in pair_copies(seg, q):
             c.wait()
-        slot = 2 * (p % (SLOTS // 2))
-        gate = jnp.dot(act[...], wbuf[slot], preferred_element_type=f32)
-        up = jnp.dot(act[...], wbuf[slot + 1], preferred_element_type=f32)
-        hid[:, pl.ds(pl.multiple_of(p * WIDE, WIDE), WIDE)] = (gate * (1.0 / (1.0 + jnp.exp(-gate))) * up).astype(bf16)
-
-        @pl.when(p + SLOTS // 2 < pairs)
-        def _():
-            pair_start(p + SLOTS // 2)
-
-        for late in range(pairs - SLOTS // 2, pairs):
-            @pl.when(p == late)
+        gate = jnp.dot(act[...], pair_ref(seg, q, 0)[...], preferred_element_type=f32)
+        up = jnp.dot(act[...], pair_ref(seg, q, 1)[...], preferred_element_type=f32)
+        hid[:, pl.ds(pl.multiple_of((segments[seg] + q) * WIDE, WIDE), WIDE)] = (
+            gate * (1.0 / (1.0 + jnp.exp(-gate))) * up).astype(bf16)
+        if seg == 0:
+            @pl.when(q < again)
             def _():
-                at = in_kv + 2 * per_slot * (late - (pairs - SLOTS // 2))
-                for b in range(at, min(at + 2 * per_slot, len(order))):
-                    down_copy(b).start()
+                pair_start(2, q)
+
+        for (s_, q_), blocks in [(key, blocks) for key, blocks in after.items() if key]:
+            if s_ == seg and len(blocks):
+                @pl.when(q == q_)
+                def _():
+                    for b in blocks:
+                        down_copy(b).start()
 
         return carry
 
-    lax.fori_loop(0, pairs, expand, 0)
-
-    def send2l(m, j):
+    for seg in range(3):
+        lax.fori_loop(0, segments[seg + 1] - segments[seg], functools.partial(expand, seg), 0)
+
+    def send2(half, role, j):
         w = pl.ds(0, widths[j])
-        return remote(s2l.at[m, j, :, w], r2l.at[m, j, :, w], s2l_s.at[m, j], s2l_r.at[m, j], left)
-
-    def send2r(m, j):
-        w = pl.ds(0, widths[j])
-        return remote(s2r.at[m, j, :, w], r2r.at[m, j, :, w], s2r_s.at[m, j], s2r_r.at[m, j], right)
+        return remote(s2.at[role, j, :, w], r2.at[role, j, :, w], s2_s.at[role, j], s2_r.at[role, j],
+                      at(turn[half] * target_at[role]))
+
+    def whole(o, j):
+        return ybuf.at[:, pl.ds(column(o, j), widths[j])]
 
     def gather2r(hop, j):
-        ref = ybuf.at[:, pl.ds(column(lax.rem(me + n - hop, n), j), widths[j])]
+        ref = whole(at(-hop), j)
         return remote(ref, ref, g2r_s.at[hop, j], g2r_r.at[hop, j], right)
 
     def gather2l(hop, j):
-        ref = ybuf.at[:, pl.ds(column(lax.rem(me + hop, n), j), widths[j])]
+        ref = whole(at(hop), j)
         return remote(ref, ref, g2l_s.at[hop, j], g2l_r.at[hop, j], left)
 
+    t_ = turn[1]
+    messages = ((0, 1), (0, -1), (0, 2), (0, -2), (-2 * t_, t_), (-2 * t_, 2 * t_), (2 * t_, -t_))
+    comes = [block - to for block, to in messages]
+
+    def gather3(c, j):
+        ref = whole(at(messages[c][0]), j)
+        return remote(ref, ref, g3_s.at[c, j - halves[1][0]], g3_r.at[c, j - halves[1][0]], at(messages[c][1]))
+
     def out_copy(k, j):
-        cols = pl.ds(column(lax.rem(me + k, n), j), widths[j])
-        return pltpu.make_async_copy(ybuf.at[:, cols], y_ref.at[:, cols], ysem.at[k, j])
-
-    def place(i):
-        return ("l", (i + 1) // 2) if i % 2 == 1 or i == 0 else ("r", i // 2 - 1)
-
-    steps, at = [], 0
-    for ph in phases:
-        for j in range(len(widths)):
-            steps.append((ph, j, list(range(at, at + len(ph)))))
-            at += len(ph)
-    for t in range(len(steps) + 1):
-        now = steps[t] if t < len(steps) else None
-        last = steps[t - 1] if t > 0 else None
-        if now:
-            for b in now[2]:
-                down_copy(b).wait()
-        if last:
-            j = last[1]
-            for i in last[0]:
-                if i == n - 1:
-                    send2l(hl - 1, j).wait_recv()
-                    send2r(hr - 1, j).wait_recv()
-                else:
-                    side, m = place(i)
-                    if m > 0:
-                        (send2l if side == "l" else send2r)(m - 1, j).wait_recv()
-        terms = []
-        if now:
-            w = widths[now[1]]
-            for b in now[2]:
-                if len(now[2]) == 2:
-                    terms.append(jnp.dot(hid[...], down_place(b)[:, 0:w], preferred_element_type=f32))
-                else:
-                    terms.append(jnp.dot(hid[:, :ff // 2], down_place(b)[:ff // 2, 0:w], preferred_element_type=f32)
-                                 + jnp.dot(hid[:, ff // 2:], down_place(b)[ff // 2:, 0:w], preferred_element_type=f32))
-        if last:
-            j, w = last[1], widths[last[1]]
-            for a, i in enumerate(last[0]):
-                s = tbuf[(t - 1) % 2, a, :, 0:w]
-                if i == n - 1:
-                    s = s + r2l[hl - 1, j, :, 0:w].astype(f32) + r2r[hr - 1, j, :, 0:w].astype(f32)
-                    cols = pl.ds(column(me, j), w)
-                    ybuf[:, cols] = (hbuf[:, :, cols].astype(f32).reshape(rows, w) + s).astype(bf16)
-                else:
-                    side, m = place(i)
-                    src, got = (s2l, r2l) if side == "l" else (s2r, r2r)
-                    if m > 0:
-                        s = s + got[m - 1, j, :, 0:w].astype(f32)
-                    src[m, j, :, 0:w] = s.astype(bf16)
-        for a, s in enumerate(terms):
-            tbuf[t % 2, a, :, 0:widths[now[1]]] = s
-        if last:
-            for i in last[0]:
-                if i == n - 1:
-                    gather2r(0, j).start()
-                    gather2l(0, j).start()
-                    out_copy(0, j).start()
-                else:
-                    side, m = place(i)
-                    (send2l if side == "l" else send2r)(m, j).start()
-
-    for hop in range(hl):
-        for j in range(len(widths)):
+        cols = pl.ds(column(at(k), j), widths[j])
+        return pltpu.make_async_copy(ybuf.at[:, cols], y_ref.at[:, cols], ysem.at[k % n, j])
+
+    def hop_on(hop):
+        for j in halves[0]:
             gather2r(hop, j).wait_recv()
             if hop + 1 < hl:
                 gather2r(hop + 1, j).start()
-            out_copy(n - 1 - hop, j).start()
+            out_copy(-1 - hop, j).start()
             if hop < hr:
                 gather2l(hop, j).wait_recv()
                 if hop + 1 < hr:
                     gather2l(hop + 1, j).start()
                 out_copy(hop + 1, j).start()
 
+    for t in range(len(steps) + 1):
+        now = steps[t] if t < len(steps) else None
+        last = steps[t - 1] if t > 0 else None
+        if now:
+            for b in (2 * t, 2 * t + 1):
+                down_copy(b).wait()
+        else:
+            hop_on(0)
+        if last:
+            for role in needs.get(last[1], ()):
+                for j in halves[last[0]]:
+                    send2(last[0], role, j).wait_recv()
+        terms = []
+        if now:
+            for b, j in zip((2 * t, 2 * t + 1), halves[now[0]]):
+                terms.append(jnp.dot(hid[...], places[b][:, 0:widths[j]], preferred_element_type=f32))
+        if last:
+            half, role = last
+            for a, j in enumerate(halves[half]):
+                w = widths[j]
+                s = tbuf[(t - 1) % 2, a, :, 0:w]
+                for r in needs.get(role, ()):
+                    s = s + r2[r, j, :, 0:w].astype(f32)
+                if role == own:
+                    cols = pl.ds(column(me, j), w)
+                    ybuf[:, cols] = (hbuf[:, :, cols].astype(f32).reshape(rows, w) + s).astype(bf16)
+                else:
+                    s2[role, j, :, 0:w] = s.astype(bf16)
+        if now:
+            for a, (j, s) in enumerate(zip(halves[now[0]], terms)):
+                tbuf[t % 2, a, :, 0:widths[j]] = s
+        if last:
+            for j in halves[half]:
+                if role != own:
+                    send2(half, role, j).start()
+                elif half == 0:
+                    gather2r(0, j).start()
+                    gather2l(0, j).start()
+                else:
+                    for c in range(4):
+                        gather3(c, j).start()
+                if role == own:
+                    out_copy(0, j).start()
+
+    hop_on(1)
+    relayed = {}
+    for c, (block, to) in enumerate(messages):
+        if block:
+            relayed.setdefault(block, []).append(c)
+    for j in halves[1]:
+        for block, on in relayed.items():
+            c = comes.index(block)
+            gather3(c, j).wait_recv()
+            for m in on:
+                gather3(m, j).start()
+            out_copy(block, j).start()
+    for j in halves[1]:
+        for c in range(2):
+            gather3(c, j).wait_recv()
+            out_copy(comes[c], j).start()
+    hop_on(2)
+    for j in halves[1]:
+        for c in range(4, len(messages)):
+            gather3(c, j).wait_recv()
+            out_copy(comes[c], j).start()
+    hop_on(3)
+
     for m in range(hl):
         send1l(m).wait_send()
-        for j in range(len(widths)):
-            send2l(m, j).wait_send()
     for m in range(hr):
         send1r(m).wait_send()
-        for j in range(len(widths)):
-            send2r(m, j).wait_send()
     for hop in range(hl):
         for s in range(subs):
             gather1r(hop, s).wait_send()
-        for j in range(len(widths)):
-            gather2r(hop, j).wait_send()
     for hop in range(hr):
         for s in range(subs):
             gather1l(hop, s).wait_send()
-        for j in range(len(widths)):
+    for half in range(2):
+        for j in halves[half]:
+            for role in range(own):
+                send2(half, role, j).wait_send()
+    for j in halves[0]:
+        for hop in range(hl):
+            gather2r(hop, j).wait_send()
+        for hop in range(hr):
             gather2l(hop, j).wait_send()
+    for j in halves[1]:
+        for c in range(len(messages)):
+            gather3(c, j).wait_send()
     for k in range(n):
         for j in range(len(widths)):
             out_copy(k, j).wait()
@@ -498,18 +560,17 @@
                 pltpu.VMEM((hr, per, dim), bf16),
                 pltpu.VMEM((hl + 1, per, dim), bf16),
                 pltpu.VMEM((hr + 1, per, dim), bf16),
-                pltpu.VMEM((hl, pieces, rows, WIDE), bf16),
-                pltpu.VMEM((hr, pieces, rows, WIDE), bf16),
-                pltpu.VMEM((hl, pieces, rows, WIDE), bf16),
-                pltpu.VMEM((hr, pieces, rows, WIDE), bf16),
+                pltpu.VMEM((n - 1, pieces, rows, WIDE), bf16),
+                pltpu.VMEM((n - 1, pieces, rows, WIDE), bf16),
                 dma((SLOTS,)),
+                dma((2 * (ff // WIDE),)),
                 dma((KV_RING,)),
                 dma((KV_RING,)),
                 dma((n * pieces,)),
                 dma((n, pieces)),
                 dma((hl,)), dma((hl,)), dma((hr,)), dma((hr,)),
                 dma((hr, 4)), dma((hr, 4)), dma((hl, 4)), dma((hl, 4)),
-                dma((hl, pieces)), dma((hl, pieces)), dma((hr, pieces)), dma((hr, pieces)),
+                dma((n - 1, pieces)), dma((n - 1, pieces)), dma((n - 1, 2)), dma((n - 1, 2)),
                 dma((hr, pieces)), dma((hr, pieces)), dma((hl, pieces)), dma((hl, pieces)),
             ],
             compiler_params=pltpu.CompilerParams(

time: 114 us -> 110 us (0.965)
  Pallas kernels: 112 us -> 108 us
    pallas_call x1, Pallas kernels: 112 us -> 108 us  [step(): pl.pallas_call(functools.partial(kernel, n, 'tp'), out_shape=jax.ShapeDty...]
where the time goes in v3:
time: 110 us
  Pallas kernels  108 us (98%)
  local copies, waits for them, and re-layouts  2.16 us (2%)
    pallas_call x1, Pallas kernels, step(): pl.pallas_call(functools.partial(kernel, n, 'tp'), out_shape=jax.ShapeDty...  108 us

profile of v3, /device:TPU:30, one launch (start us, length us, event | category | flops | bytes accessed | tf_op | source)
XLA Modules:
  0.0 110.0 jit_solution(15596898206060480660)
XLA Ops:
  0.0 107.9 %layer.1 = bf16[64,7168]{1,0:T(8,128)(2,1)} custom-call(bf16[8,8,7168]{2,1,0:T(8,128)(2,1)} %bitcast.7, f32[2,128]{1,0:T(2,128)} %constant.2.clone.rot_ref, bf16[56,128]{1,0:T(8,128)(2,1)} %bitcast.8, bf16[56,128]{1,0:T(8,128)(2,1)} %bitcast.9, bf16[64,2048,128]{2,1,0:T(8,128)(2,1)} %bitcast.5, bf16[64,2048,128]{2,1,0:T(8,128)(2,1)} %bitcast.6, ...), custom_call_target="tpu_custom_call" | custom-call | tf_op jit(solution)/shard_map/layer/pallas_call | solution.py:541
  107.9 2.2 %copy.13 = bf16[64,7168]{1,0:T(8,128)(2,1)} copy(bf16[64,7168]{1,0:T(8,128)(2,1)} %layer.1) | data formatting | bytes 1835008

commit v4 on v3

--- a/solution.py
+++ b/solution.py
@@ -116,7 +116,7 @@
     target_at = (-2, -1, 1, -1, 1, -2, 2)
     needs = {near2: (far, near3), other2: (other3,), own: (near1, other1, near2, other2)}
     steps = [(0, far), (0, near3), (0, other3), (1, far), (1, near3), (1, other3), (0, near1), (0, other1),
-             (0, near2), (0, other2), (1, near1), (1, other1), (0, own), (1, near2), (1, other2), (1, own)]
+             (0, near2), (0, other2), (1, near1), (1, other1), (1, near2), (1, other2), (0, own), (1, own)]
     order = [(half, role, j) for half, role in steps for j in halves[half]]
 
     def at(shift):
@@ -350,15 +350,17 @@
         gather1l(0, s).start()
     for b in after[None]:
         down_copy(b).start()
+
+    def goes(side, hop, first):
+        return hop < hr or (hop == hr and first == (side > 0))
+
     for hop in range(hl):
         for s in range(subs):
-            gather1r(hop, s).wait_recv()
-            if hop + 1 < hl:
-                gather1r(hop + 1, s).start()
-            if hop < hr:
-                gather1l(hop, s).wait_recv()
-                if hop + 1 < hr:
-                    gather1l(hop + 1, s).start()
+            for side, gather in ((1, gather1r), (-1, gather1l)):
+                if goes(side, hop, s < subs // 2):
+                    gather(hop, s).wait_recv()
+                    if goes(side, hop + 1, s < subs // 2):
+                        gather(hop + 1, s).start()
 
     normed_into(lambda r, l: hbuf[r, :, l * HEAD:(l + 1) * HEAD].astype(f32), gain_m_ref)
 
@@ -416,15 +418,12 @@
 
     def hop_on(hop):
         for j in halves[0]:
-            gather2r(hop, j).wait_recv()
-            if hop + 1 < hl:
-                gather2r(hop + 1, j).start()
-            out_copy(-1 - hop, j).start()
-            if hop < hr:
-                gather2l(hop, j).wait_recv()
-                if hop + 1 < hr:
-                    gather2l(hop + 1, j).start()
-                out_copy(hop + 1, j).start()
+            for side, gather in ((1, gather2r), (-1, gather2l)):
+                if goes(side, hop, j == halves[0][0]):
+                    gather(hop, j).wait_recv()
+                    if goes(side, hop + 1, j == halves[0][0]):
+                        gather(hop + 1, j).start()
+                    out_copy(-side * (hop + 1), j).start()
 
     for t in range(len(steps) + 1):
         now = steps[t] if t < len(steps) else None
@@ -432,8 +431,6 @@
         if now:
             for b in (2 * t, 2 * t + 1):
                 down_copy(b).wait()
-        else:
-            hop_on(0)
         if last:
             for role in needs.get(last[1], ()):
                 for j in halves[last[0]]:
@@ -470,11 +467,12 @@
                 if role == own:
                     out_copy(0, j).start()
 
-    hop_on(1)
     relayed = {}
     for c, (block, to) in enumerate(messages):
         if block:
             relayed.setdefault(block, []).append(c)
+    hop_on(0)
+    hop_on(1)
     for j in halves[1]:
         for block, on in relayed.items():
             c = comes.index(block)
@@ -498,20 +496,18 @@
     for m in range(hr):
         send1r(m).wait_send()
     for hop in range(hl):
-        for s in range(subs):
-            gather1r(hop, s).wait_send()
-    for hop in range(hr):
-        for s in range(subs):
-            gather1l(hop, s).wait_send()
+        for side, gather in ((1, gather1r), (-1, gather1l)):
+            for s in range(subs):
+                if goes(side, hop, s < subs // 2):
+                    gather(hop, s).wait_send()
+        for side, gather in ((1, gather2r), (-1, gather2l)):
+            for j in halves[0]:
+                if goes(side, hop, j == halves[0][0]):
+                    gather(hop, j).wait_send()
     for half in range(2):
         for j in halves[half]:
             for role in range(own):
                 send2(half, role, j).wait_send()
-    for j in halves[0]:
-        for hop in range(hl):
-            gather2r(hop, j).wait_send()
-        for hop in range(hr):
-            gather2l(hop, j).wait_send()
     for j in halves[1]:
         for c in range(len(messages)):
             gather3(c, j).wait_send()
@@ -569,9 +565,9 @@
                 dma((n * pieces,)),
                 dma((n, pieces)),
                 dma((hl,)), dma((hl,)), dma((hr,)), dma((hr,)),
-                dma((hr, 4)), dma((hr, 4)), dma((hl, 4)), dma((hl, 4)),
+                dma((hl, 4)), dma((hl, 4)), dma((hl, 4)), dma((hl, 4)),
                 dma((n - 1, pieces)), dma((n - 1, pieces)), dma((n - 1, 2)), dma((n - 1, 2)),
-                dma((hr, pieces)), dma((hr, pieces)), dma((hl, pieces)), dma((hl, pieces)),
+                dma((hl, pieces)), dma((hl, pieces)), dma((hl, pieces)), dma((hl, pieces)),
             ],
             compiler_params=pltpu.CompilerParams(
                 collective_id=0, has_side_effects=True, vmem_limit_bytes=67043328),

time: 110 us -> 109 us (level)
    pallas_call x1, Pallas kernels: 108 us -> 107 us  [step(): pl.pallas_call(functools.partial(kernel, n, 'tp'), out_shape=jax.ShapeDty...]
where the time goes in v4:
time: 109 us
  Pallas kernels  107 us (98%)
  local copies, waits for them, and re-layouts  2.16 us (2%)
    pallas_call x1, Pallas kernels, step(): pl.pallas_call(functools.partial(kernel, n, 'tp'), out_shape=jax.ShapeDty...  107 us

profile of v4, /device:TPU:30, one launch (start us, length us, event | category | flops | bytes accessed | tf_op | source)
XLA Modules:
  0.0 108.8 jit_solution(18075138754561880965)
XLA Ops:
  0.0 106.6 %layer.1 = bf16[64,7168]{1,0:T(8,128)(2,1)} custom-call(bf16[8,8,7168]{2,1,0:T(8,128)(2,1)} %bitcast.7, f32[2,128]{1,0:T(2,128)} %constant.2.clone.rot_ref, bf16[56,128]{1,0:T(8,128)(2,1)} %bitcast.8, bf16[56,128]{1,0:T(8,128)(2,1)} %bitcast.9, bf16[64,2048,128]{2,1,0:T(8,128)(2,1)} %bitcast.5, bf16[64,2048,128]{2,1,0:T(8,128)(2,1)} %bitcast.6, ...), custom_call_target="tpu_custom_call" | custom-call | tf_op jit(solution)/shard_map/layer/pallas_call | solution.py:537
  106.7 2.2 %copy.13 = bf16[64,7168]{1,0:T(8,128)(2,1)} copy(bf16[64,7168]{1,0:T(8,128)(2,1)} %layer.1) | data formatting | bytes 1835008

commit v5 on v4

--- a/solution.py
+++ b/solution.py
@@ -29,7 +29,7 @@
            s1l, s1r, r1l, r1r, s2, r2,
            wsem, gsem, ksem, vsem, dsem, ysem,
            s1l_s, s1l_r, s1r_s, s1r_r, g1l_s, g1l_r, g1r_s, g1r_r,
-           s2_s, s2_r, g3_s, g3_r, g2l_s, g2l_r, g2r_s, g2r_r):
+           s2_s, s2_r, g2l_s, g2l_r, g2r_s, g2r_r):
     me = lax.axis_index(axis)
     right, left = lax.rem(me + 1, n), lax.rem(me + n - 1, n)
     rows, dim = act.shape
@@ -52,7 +52,7 @@
         return lax.rem(me + k, n)
 
     barrier = pltpu.get_barrier_semaphore()
-    for other in (left, right, lax.rem(me + 2, n), lax.rem(me + n - 2, n)):
+    for other in (left, right):
         pl.semaphore_signal(barrier, inc=1, device_id={axis: other}, device_id_type=MESH)
 
     def wq_copy(b):
@@ -113,10 +113,10 @@
     turn = (1, -1)
     far, near3, other3, near1, other1, near2, other2, own = range(8)
     owner_at = (4, -3, 3, -1, 1, -2, 2, 0)
-    target_at = (-2, -1, 1, -1, 1, -2, 2)
-    needs = {near2: (far, near3), other2: (other3,), own: (near1, other1, near2, other2)}
-    steps = [(0, far), (0, near3), (0, other3), (1, far), (1, near3), (1, other3), (0, near1), (0, other1),
-             (0, near2), (0, other2), (1, near1), (1, other1), (1, near2), (1, other2), (0, own), (1, own)]
+    target_at = (-1, -1, 1, -1, 1, -1, 1)
+    needs = {near3: (far,), near2: (near3,), other2: (other3,), near1: (near2,), other1: (other2,),
+             own: (near1, other1)}
+    steps = [(half, role) for role in (far, other3, near3, other2, near2, other1, near1, own) for half in range(2)]
     order = [(half, role, j) for half, role in steps for j in halves[half]]
 
     def at(shift):
@@ -203,7 +203,7 @@
                 h = c * (WIDE // HEAD) + s
                 qh[h * rows:(h + 1) * rows, :] = turned.astype(bf16).astype(f32)
     qh[heads * rows:, :] = jnp.zeros((qh.shape[0] - heads * rows, HEAD), f32)
-    pl.semaphore_wait(barrier, 4)
+    pl.semaphore_wait(barrier, 2)
 
     def scores(it, s_ref):
         row = first_row(it)
@@ -404,24 +404,16 @@
         ref = whole(at(hop), j)
         return remote(ref, ref, g2l_s.at[hop, j], g2l_r.at[hop, j], left)
 
-    t_ = turn[1]
-    messages = ((0, 1), (0, -1), (0, 2), (0, -2), (-2 * t_, t_), (-2 * t_, 2 * t_), (2 * t_, -t_))
-    comes = [block - to for block, to in messages]
-
-    def gather3(c, j):
-        ref = whole(at(messages[c][0]), j)
-        return remote(ref, ref, g3_s.at[c, j - halves[1][0]], g3_r.at[c, j - halves[1][0]], at(messages[c][1]))
-
     def out_copy(k, j):
         cols = pl.ds(column(at(k), j), widths[j])
         return pltpu.make_async_copy(ybuf.at[:, cols], y_ref.at[:, cols], ysem.at[k % n, j])
 
     def hop_on(hop):
-        for j in halves[0]:
+        for j in range(len(widths)):
             for side, gather in ((1, gather2r), (-1, gather2l)):
-                if goes(side, hop, j == halves[0][0]):
+                if goes(side, hop, j % 2 == 0):
                     gather(hop, j).wait_recv()
-                    if goes(side, hop + 1, j == halves[0][0]):
+                    if goes(side, hop + 1, j % 2 == 0):
                         gather(hop + 1, j).start()
                     out_copy(-side * (hop + 1), j).start()
 
@@ -458,38 +450,13 @@
             for j in halves[half]:
                 if role != own:
                     send2(half, role, j).start()
-                elif half == 0:
+                else:
                     gather2r(0, j).start()
                     gather2l(0, j).start()
-                else:
-                    for c in range(4):
-                        gather3(c, j).start()
-                if role == own:
                     out_copy(0, j).start()
 
-    relayed = {}
-    for c, (block, to) in enumerate(messages):
-        if block:
-            relayed.setdefault(block, []).append(c)
-    hop_on(0)
-    hop_on(1)
-    for j in halves[1]:
-        for block, on in relayed.items():
-            c = comes.index(block)
-            gather3(c, j).wait_recv()
-            for m in on:
-                gather3(m, j).start()
-            out_copy(block, j).start()
-    for j in halves[1]:
-        for c in range(2):
-            gather3(c, j).wait_recv()
-            out_copy(comes[c], j).start()
-    hop_on(2)
-    for j in halves[1]:
-        for c in range(4, len(messages)):
-            gather3(c, j).wait_recv()
-            out_copy(comes[c], j).start()
-    hop_on(3)
+    for hop in range(hl):
+        hop_on(hop)
 
     for m in range(hl):
         send1l(m).wait_send()
@@ -501,16 +468,13 @@
                 if goes(side, hop, s < subs // 2):
                     gather(hop, s).wait_send()
         for side, gather in ((1, gather2r), (-1, gather2l)):
-            for j in halves[0]:
-                if goes(side, hop, j == halves[0][0]):
+            for j in range(len(widths)):
+                if goes(side, hop, j % 2 == 0):
                     gather(hop, j).wait_send()
     for half in range(2):
         for j in halves[half]:
             for role in range(own):
                 send2(half, role, j).wait_send()
-    for j in halves[1]:
-        for c in range(len(messages)):
-            gather3(c, j).wait_send()
     for k in range(n):
         for j in range(len(widths)):
             out_copy(k, j).wait()
@@ -566,7 +530,7 @@
                 dma((n, pieces)),
                 dma((hl,)), dma((hl,)), dma((hr,)), dma((hr,)),
                 dma((hl, 4)), dma((hl, 4)), dma((hl, 4)), dma((hl, 4)),
-                dma((n - 1, pieces)), dma((n - 1, pieces)), dma((n - 1, 2)), dma((n - 1, 2)),
+                dma((n - 1, pieces)), dma((n - 1, pieces)),
                 dma((hl, pieces)), dma((hl, pieces)), dma((hl, pieces)), dma((hl, pieces)),
             ],
             compiler_params=pltpu.CompilerParams(

time: 109 us -> 111 us (1.018)
    pallas_call x1, Pallas kernels: 107 us -> 108 us  [step(): pl.pallas_call(functools.partial(kernel, n, 'tp'), out_shape=jax.ShapeDty...]
where the time goes in v5:
time: 111 us
  Pallas kernels  108 us (97%)
  local copies, waits for them, and re-layouts  2.16 us (2%)
    pallas_call x1, Pallas kernels, step(): pl.pallas_call(functools.partial(kernel, n, 'tp'), out_shape=jax.ShapeDty...  108 us

profile of v5, /device:TPU:30, one launch (start us, length us, event | category | flops | bytes accessed | tf_op | source)
XLA Modules:
  0.0 110.6 jit_solution(15076627976538783621)
XLA Ops:
  0.0 108.4 %layer.1 = bf16[64,7168]{1,0:T(8,128)(2,1)} custom-call(bf16[8,8,7168]{2,1,0:T(8,128)(2,1)} %bitcast.7, f32[2,128]{1,0:T(2,128)} %constant.2.clone.rot_ref, bf16[56,128]{1,0:T(8,128)(2,1)} %bitcast.8, bf16[56,128]{1,0:T(8,128)(2,1)} %bitcast.9, bf16[64,2048,128]{2,1,0:T(8,128)(2,1)} %bitcast.5, bf16[64,2048,128]{2,1,0:T(8,128)(2,1)} %bitcast.6, ...), custom_call_target="tpu_custom_call" | custom-call | tf_op jit(solution)/shard_map/layer/pallas_call | solution.py:501
  108.4 2.2 %copy.13 = bf16[64,7168]{1,0:T(8,128)(2,1)} copy(bf16[64,7168]{1,0:T(8,128)(2,1)} %layer.1) | data formatting | bytes 1835008

commit v6 on v4

--- a/solution.py
+++ b/solution.py
@@ -24,10 +24,10 @@
     return 4 + odd * ((k + 1) // 2) - (1 - odd) * (k // 2)
 
 
-def kernel(n, axis, x_ref, rot_ref, gain_a_ref, gain_m_ref, k_ref, v_ref, wq_ref, wo_ref, wg_ref, wu_ref, wd_ref, y_ref,
-           kv, wbuf, act, hbuf, ybuf, term, hid, qh, oh, sa, sb, tbuf,
+def kernel(n, axis, x_hbm, rot_ref, gain_a_ref, gain_m_ref, k_ref, v_ref, wq_ref, wo_ref, wg_ref, wu_ref, wd_ref, y_ref,
+           kv, wbuf, x_ref, act, hbuf, ybuf, term, hid, qh, oh, sa, sb, tbuf,
            s1l, s1r, r1l, r1r, s2, r2,
-           wsem, gsem, ksem, vsem, dsem, ysem,
+           xsem, wsem, gsem, ksem, vsem, dsem, ysem,
            s1l_s, s1l_r, s1r_s, s1r_r, g1l_s, g1l_r, g1r_s, g1r_r,
            s2_s, s2_r, g3_s, g3_r, g2l_s, g2l_r, g2r_s, g2r_r):
     me = lax.axis_index(axis)
@@ -158,8 +158,11 @@
             wd_ref.at[:, pl.ds(column(at(turn[half] * owner_at[role]), j), w)],
             places[b].at[:, pl.ds(0, w)], dsem.at[b])
 
+    x_copy = pltpu.make_async_copy(x_hbm, x_ref, xsem.at[0])
+    x_copy.start()
     for b in range(q_blocks):
         wq_copy(b).start()
+    x_copy.wait()
 
     def normed_into(read, gain_ref):
         def group(g, carry):
@@ -271,7 +274,7 @@
         return remote(s1r.at[m], r1r.at[m + 1], s1r_s.at[m], s1r_r.at[m], right)
 
     strips = [slice(c, c + own_cols) for c in range(0, dim, own_cols)]
-    body = wo_blocks // 2
+    body = wo_blocks
 
     def phase(p, carry):
         lax.fori_loop(jnp.maximum(0, 2 * p - 1), jnp.minimum(n, 2 * p + 1), attend, 0)
@@ -537,11 +540,12 @@
         return pl.pallas_call(
             functools.partial(kernel, n, "tp"),
             out_shape=jax.ShapeDtypeStruct((rows, dim), bf16),
-            in_specs=[inside] * 4 + [anywhere] * 7,
+            in_specs=[anywhere] + [inside] * 3 + [anywhere] * 7,
             out_specs=anywhere,
             scratch_shapes=[
                 pltpu.VMEM((KV_RING * 4 * cache, WIDE), bf16),
                 pltpu.VMEM((SLOTS, dim, WIDE), bf16),
+                pltpu.VMEM((n, per, dim), bf16),
                 pltpu.VMEM((rows, dim), bf16),
                 pltpu.VMEM((n, per, dim), bf16),
                 pltpu.VMEM((rows, dim), bf16),
@@ -558,6 +562,7 @@
                 pltpu.VMEM((hr + 1, per, dim), bf16),
                 pltpu.VMEM((n - 1, pieces, rows, WIDE), bf16),
                 pltpu.VMEM((n - 1, pieces, rows, WIDE), bf16),
+                dma((1,)),
                 dma((SLOTS,)),
                 dma((2 * (ff // WIDE),)),
                 dma((KV_RING,)),

time: 109 us -> 109 us (level)
  no operation moved by 1% of the time
where the time goes in v6:
time: 109 us; the launch traced here: 108 us
  Pallas kernels  106 us (97%)
  local copies, waits for them, and re-layouts  2.16 us (2%)
    pallas_call x1, Pallas kernels, step(): pl.pallas_call(functools.partial(kernel, n, 'tp'), out_shape=jax.ShapeDty...  106 us

profile of v6, /device:TPU:30, one launch (start us, length us, event | category | flops | bytes accessed | tf_op | source)
XLA Modules:
  0.0 108.2 jit_solution(3700261803312258812)
XLA Ops:
  0.0 106.0 %layer.1 = bf16[64,7168]{1,0:T(8,128)(2,1)} custom-call(bf16[8,8,7168]{2,1,0:T(8,128)(2,1)} %bitcast.7, f32[2,128]{1,0:T(2,128)} %constant.2.clone.rot_ref, bf16[56,128]{1,0:T(8,128)(2,1)} %bitcast.8, bf16[56,128]{1,0:T(8,128)(2,1)} %bitcast.9, bf16[64,2048,128]{2,1,0:T(8,128)(2,1)} %bitcast.5, bf16[64,2048,128]{2,1,0:T(8,128)(2,1)} %bitcast.6, ...), custom_call_target="tpu_custom_call" | custom-call | tf_op jit(solution)/shard_map/layer/pallas_call | solution.py:540
  106.0 2.2 %copy.13 = bf16[64,7168]{1,0:T(8,128)(2,1)} copy(bf16[64,7168]{1,0:T(8,128)(2,1)} %layer.1) | data formatting | bytes 1835008
